TPU v7x, 32 devices: a whole 2x2x4 slice. The times are simulated.
32 devices in a mesh: rep: 4 (over x, core), shard: 8 (over z, y).
Axes of the slice: x: 2, y: 2, z: 4, core: 2. Of those that a mesh axis runs over, the one named last changes fastest.
Arguments:
- images: bfloat16 [32, 256, 1152], P(('rep', 'shard')), may hold values from -6 to 6
- cotangent: bfloat16 [32, 256, 1152], P(('rep', 'shard')), may hold values from -6 to 6
- w_qkv: bfloat16 [1152, 3456], P('shard'), may hold values from -2 to 2
- w_out: bfloat16 [1152, 1152], P('shard'), may hold values from -0.75 to 0.75
- w_up: bfloat16 [1152, 4304], P('shard'), may hold values from -0.1875 to 0.1875
- w_down: bfloat16 [1152, 4304], P('shard'), may hold values from -0.125 to 0.125
- vectors: bfloat16 [1152, 8], P('shard'), may hold values from -3 to 3, as said below
- up_bias: bfloat16 [4304], replicated, may hold values from -3 to 3
Outputs:
- outputs: bfloat16 [32, 256, 1152], P(('rep', 'shard'))
- input_grad: bfloat16 [32, 256, 1152], P(('rep', 'shard'))
- qkv_grad: float32 [1152, 3456], P('shard')
- out_grad: float32 [1152, 1152], P('shard')
- up_grad: float32 [1152, 4304], P('shard')
- down_grad: float32 [1152, 4304], P('shard')
- vectors_grad: float32 [1152, 8], P('shard')
- up_bias_grad: float32 [4304], replicated
Inputs may be any that keep to these rules, and one draw needn't show every extreme that they name: `vectors`: columns 0 and 5 (the norms' gains) are positive; the other columns have either sign.
All inputs are finite; a program needn't handle non-finite values.
Results may differ from a plain program's by a relative error of at most 0.014.
Values may be sent and summed in bfloat16 or wider, within the bound.
A program may use at most 256 MiB of HBM per device.

v0:
```python
import math

import jax
import jax.numpy as jnp
from jax import lax
from jax.sharding import PartitionSpec as P

HEAD_DIM = 72


EPSILON = 1e-06
GELU_COEF = 0.044715
ROOT_TWO_PI = math.sqrt(2.0 / math.pi)


def batched(pattern, left_op, right_op):
    return jnp.einsum(pattern, left_op, right_op, preferred_element_type=jnp.float32)


def contract_rows(left_op, right_op):
    return lax.dot_general(
        left_op, right_op, (((0,), (0,)), ((), ())), preferred_element_type=jnp.float32
    )


def contract_cols(left_op, right_op):
    return lax.dot_general(
        left_op, right_op, (((1,), (1,)), ((), ())), preferred_element_type=jnp.float32
    )


def norm_rows(hidden):
    row_mean = jnp.mean(hidden, axis=-1, keepdims=True)
    centered = hidden - row_mean
    variance = jnp.mean(centered * centered, axis=-1, keepdims=True)
    inv_std = lax.rsqrt(variance + EPSILON)
    return (centered * inv_std, inv_std)


def norm_back(grad_normed, normed, inv_std):
    mean_grad = jnp.mean(grad_normed, axis=-1, keepdims=True)
    mean_proj = jnp.mean(grad_normed * normed, axis=-1, keepdims=True)
    return inv_std * (grad_normed - mean_grad - normed * mean_proj)


def gelu_parts(pre_act):
    tanh_term = jnp.tanh(ROOT_TWO_PI * (pre_act + GELU_COEF * pre_act * pre_act * pre_act))
    activated = 0.5 * pre_act * (1.0 + tanh_term)
    derivative = 0.5 * (1.0 + tanh_term) + 0.5 * pre_act * (
        1.0 - tanh_term * tanh_term
    ) * ROOT_TWO_PI * (1.0 + 3.0 * GELU_COEF * pre_act * pre_act)
    return (activated, derivative)


def split_heads(tensor, batch_count, seq_len, head_size):
    return tensor.reshape(batch_count, seq_len, tensor.shape[-1] // head_size, head_size)


def forward_pass(images, w_qkv, w_out, w_up, w_down, vectors, up_bias):
    params = vectors.astype(jnp.float32)
    batch_count, seq_len, model_width = images.shape
    flat_rows = images.reshape(batch_count * seq_len, model_width).astype(jnp.float32)
    normed_one, inv_one = norm_rows(flat_rows)
    input_one = (normed_one * params[:, 0] + params[:, 1]).astype(jnp.bfloat16)
    projected = jnp.dot(input_one, w_qkv, preferred_element_type=jnp.float32)
    query = (projected[:, :model_width] + params[:, 2]).astype(jnp.bfloat16)
    keys_all = projected[:, model_width : 2 * model_width].astype(jnp.bfloat16)
    values_all = (projected[:, 2 * model_width :] + params[:, 3]).astype(jnp.bfloat16)
    score_scale = 1.0 / math.sqrt(HEAD_DIM)
    query_heads = split_heads(query, batch_count, seq_len, HEAD_DIM)
    key_heads = split_heads(keys_all, batch_count, seq_len, HEAD_DIM)
    value_heads = split_heads(values_all, batch_count, seq_len, HEAD_DIM)
    scores = batched("bqhd,bkhd->bhqk", query_heads, key_heads) * score_scale
    row_max = jnp.max(scores, axis=-1, keepdims=True)
    exponent = jnp.exp(scores - row_max)
    row_total = jnp.sum(exponent, axis=-1, keepdims=True)
    weights = (exponent / row_total).astype(jnp.bfloat16)
    logsum = row_max + jnp.log(row_total)
    attended = (
        batched("bhqk,bkhd->bqhd", weights, value_heads)
        .reshape(batch_count * seq_len, model_width)
        .astype(jnp.bfloat16)
    )
    middle = flat_rows + jnp.dot(attended, w_out, preferred_element_type=jnp.float32) + params[:, 4]
    normed_two, inv_two = norm_rows(middle)
    input_two = (normed_two * params[:, 5] + params[:, 6]).astype(jnp.bfloat16)
    pre_act = jnp.dot(input_two, w_up, preferred_element_type=jnp.float32) + up_bias.astype(
        jnp.float32
    )
    activated, derivative = gelu_parts(pre_act)
    act_bf = activated.astype(jnp.bfloat16)
    final = middle + contract_cols(act_bf, w_down) + params[:, 7]
    outputs = final.astype(jnp.bfloat16).reshape(batch_count, seq_len, model_width)
    saved = (
        normed_one,
        inv_one,
        input_one,
        query,
        keys_all,
        values_all,
        logsum,
        attended,
        normed_two,
        inv_two,
        input_two,
        derivative,
        act_bf,
    )
    return (outputs, saved)


def backward_pass(cotangent, saved, w_qkv, w_out, w_up, w_down, vectors):
    (
        normed_one,
        inv_one,
        input_one,
        query,
        keys_all,
        values_all,
        logsum,
        attended,
        normed_two,
        inv_two,
        input_two,
        derivative,
        act_bf,
    ) = saved
    params = vectors.astype(jnp.float32)
    batch_count, seq_len, model_width = cotangent.shape
    grad_bf = cotangent.reshape(batch_count * seq_len, model_width)
    grad_final = grad_bf.astype(jnp.float32)
    down_term = contract_rows(grad_bf, act_bf)
    grad_act = jnp.dot(grad_bf, w_down, preferred_element_type=jnp.float32)
    grad_pre = grad_act * derivative
    upb_term = jnp.sum(grad_pre, axis=0)
    grad_pre_bf = grad_pre.astype(jnp.bfloat16)
    up_term = contract_rows(input_two, grad_pre_bf)
    grad_two = contract_cols(grad_pre_bf, w_up)
    grad_gain_two = jnp.sum(grad_two * normed_two, axis=0)
    grad_bias_two = jnp.sum(grad_two, axis=0)
    grad_middle = grad_final + norm_back(grad_two * params[:, 5], normed_two, inv_two)
    grad_out_bias = jnp.sum(grad_middle, axis=0)
    grad_middle_bf = grad_middle.astype(jnp.bfloat16)
    out_term = contract_rows(attended, grad_middle_bf)
    grad_att = contract_cols(grad_middle_bf, w_out).astype(jnp.bfloat16)
    score_scale = 1.0 / math.sqrt(HEAD_DIM)
    query_heads = split_heads(query, batch_count, seq_len, HEAD_DIM)
    key_heads = split_heads(keys_all, batch_count, seq_len, HEAD_DIM)
    value_heads = split_heads(values_all, batch_count, seq_len, HEAD_DIM)
    grad_heads = split_heads(grad_att, batch_count, seq_len, HEAD_DIM)
    scores = batched("bqhd,bkhd->bhqk", query_heads, key_heads) * score_scale
    probs = jnp.exp(scores - logsum)
    probs_bf = probs.astype(jnp.bfloat16)
    grad_value = batched("bhqk,bqhd->bkhd", probs_bf, grad_heads)
    grad_prob = batched("bqhd,bkhd->bhqk", grad_heads, value_heads)
    delta = jnp.sum(probs * grad_prob, axis=-1, keepdims=True)
    grad_score = (probs * (grad_prob - delta) * score_scale).astype(jnp.bfloat16)
    grad_query = batched("bhqk,bkhd->bqhd", grad_score, key_heads)
    grad_key = batched("bhqk,bqhd->bkhd", grad_score, query_heads)
    flat_count = batch_count * seq_len
    grad_query = grad_query.reshape(flat_count, model_width)
    grad_key = grad_key.reshape(flat_count, model_width)
    grad_value = grad_value.reshape(flat_count, model_width)
    grad_qbias = jnp.sum(grad_query, axis=0)
    grad_vbias = jnp.sum(grad_value, axis=0)
    grad_proj = jnp.concatenate([grad_query, grad_key, grad_value], axis=1).astype(jnp.bfloat16)
    qkv_term = contract_rows(input_one, grad_proj)
    grad_one = contract_cols(grad_proj, w_qkv)
    grad_gain_one = jnp.sum(grad_one * normed_one, axis=0)
    grad_bias_one = jnp.sum(grad_one, axis=0)
    grad_input = grad_middle + norm_back(grad_one * params[:, 0], normed_one, inv_one)
    grad_down_bias = jnp.sum(grad_final, axis=0)
    vector_term = jnp.stack(
        [
            grad_gain_one,
            grad_bias_one,
            grad_qbias,
            grad_vbias,
            grad_out_bias,
            grad_gain_two,
            grad_bias_two,
            grad_down_bias,
        ],
        axis=1,
    )
    input_grad = grad_input.astype(jnp.bfloat16).reshape(batch_count, seq_len, model_width)
    return (input_grad, (qkv_term, out_term, up_term, down_term, vector_term), upb_term)


def per_device(images, cotangent, w_qkv, w_out, w_up, w_down, vectors, up_bias):
    whole = (
        lax.all_gather(w_qkv, "shard", axis=0, tiled=True),
        lax.all_gather(w_out, "shard", axis=0, tiled=True),
        lax.all_gather(w_up, "shard", axis=0, tiled=True),
        lax.all_gather(w_down, "shard", axis=0, tiled=True),
        lax.all_gather(vectors, "shard", axis=0, tiled=True),
    )
    outputs, saved = forward_pass(images, whole[0], whole[1], whole[2], whole[3], whole[4], up_bias)
    again = (
        lax.all_gather(w_qkv, "shard", axis=0, tiled=True),
        lax.all_gather(w_out, "shard", axis=0, tiled=True),
        lax.all_gather(w_up, "shard", axis=0, tiled=True),
        lax.all_gather(w_down, "shard", axis=0, tiled=True),
        lax.all_gather(vectors, "shard", axis=0, tiled=True),
    )
    input_grad, terms, upb_term = backward_pass(
        cotangent, saved, again[0], again[1], again[2], again[3], again[4]
    )
    upb_total = lax.psum(upb_term, ("rep", "shard"))
    owned = (
        lax.psum_scatter(terms[0], "shard", scatter_dimension=0, tiled=True),
        lax.psum_scatter(terms[1], "shard", scatter_dimension=0, tiled=True),
        lax.psum_scatter(terms[2], "shard", scatter_dimension=0, tiled=True),
        lax.psum_scatter(terms[3], "shard", scatter_dimension=0, tiled=True),
        lax.psum_scatter(terms[4], "shard", scatter_dimension=0, tiled=True),
    )
    parted = (
        lax.psum_scatter(owned[0], "rep", scatter_dimension=0, tiled=True),
        lax.psum_scatter(owned[1], "rep", scatter_dimension=0, tiled=True),
        lax.psum_scatter(owned[2], "rep", scatter_dimension=0, tiled=True),
        lax.psum_scatter(owned[3], "rep", scatter_dimension=0, tiled=True),
        lax.psum_scatter(owned[4], "rep", scatter_dimension=0, tiled=True),
    )
    summed = (
        lax.all_gather(parted[0], "rep", axis=0, tiled=True),
        lax.all_gather(parted[1], "rep", axis=0, tiled=True),
        lax.all_gather(parted[2], "rep", axis=0, tiled=True),
        lax.all_gather(parted[3], "rep", axis=0, tiled=True),
        lax.all_gather(parted[4], "rep", axis=0, tiled=True),
    )
    return (outputs, input_grad, summed[0], summed[1], summed[2], summed[3], summed[4], upb_total)


def solution(mesh):
    placed = (
        P(("rep", "shard"), None, None),
        P(("rep", "shard"), None, None),
        P("shard", None),
        P("shard", None),
        P("shard", None),
        P("shard", None),
        P("shard", None),
        P(),
    )
    return jax.shard_map(
        per_device,
        mesh=mesh,
        in_specs=placed,
        out_specs=(
            P(("rep", "shard"), None, None),
            P(("rep", "shard"), None, None),
            P("shard", None),
            P("shard", None),
            P("shard", None),
            P("shard", None),
            P("shard", None),
            P(),
        ),
        check_vma=False,
    )
```

profile of v0, /device:TPU:0, one launch (start us, length us, event | category | flops | bytes accessed | tf_op | source)
XLA Modules:
  0.0 1816.1 jit_solution(12791949931599254159)
XLA Ops:
  10.0 33.4 %all-gather = bf16[8,144,8]{1,2,0:T(8,128)(2,1)S(1)} all-gather(bf16[1,144,8]{1,2,0:T(8,128)(2,1)S(1)} %bitcast.145), channel_id=1, replica_groups=mesh['rep'=4,'shard'=8] {'shard'}, dimensions={0}, use_global_device_ids=true | all-gather | bytes 20736 | tf_op jit(solution)/shard_map/all_gather | solution.py:196
  45.3 86.9 %all-gather.14.cloned.1.call-done = bf16[1152,3456]{1,0:T(8,128)(2,1)} async-done(((bf16[144,3456]{1,0:T(8,128)(2,1)}), bf16[1152,3456]{1,0:T(8,128)(2,1)}) %all-gather.14.cloned.1.call-update) | async-done | bytes 7962640 | tf_op jit(solution)/shard_map/all_gather | solution.py:192
  132.2 6.0 fusion.88
  139.2 0.8 multiply_reduce_fusion.1
  140.0 0.7 fusion.10
  140.8 1.2 copy-done
  142.0 1.0 fusion.50
  143.0 44.5 %all-gather.16.cloned.1.call-done = bf16[1152,1152]{1,0:T(8,128)(2,1)} async-done(((bf16[144,1152]{1,0:T(8,128)(2,1)}), bf16[1152,1152]{1,0:T(8,128)(2,1)}) %all-gather.16.cloned.1.call-update) | async-done | bytes 2654224 | tf_op jit(solution)/shard_map/all_gather | solution.py:193
  187.6 2.9 fusion.95
  190.8 142.4 %all-gather.18.cloned.1.call-done = bf16[1152,4304]{1,0:T(8,128)(2,1)} async-done(((bf16[144,4304]{1,0:T(8,128)(2,1)}), bf16[1152,4304]{1,0:T(8,128)(2,1)}) %all-gather.18.cloned.1.call-update) | async-done | bytes 9916432 | tf_op jit(solution)/shard_map/all_gather | solution.py:194
  333.2 8.0 convolution_add_fusion
  341.2 2.0 copy-done.2
  343.2 8.7 convolution_bitcast_fusion
  351.9 21.6 %copy.63 = f32[1152,4304]{1,0:T(8,128)} copy(f32[1152,4304]{0,1:T(8,128)} %convolution_bitcast_fusion) | data formatting | bytes 39665664
  373.6 104.6 %all-gather.20.cloned.1.call-done = bf16[1152,4304]{1,0:T(8,128)(2,1)} async-done(((bf16[144,4304]{1,0:T(8,128)(2,1)}), bf16[1152,4304]{1,0:T(8,128)(2,1)}) %all-gather.20.cloned.1.call-update) | async-done | bytes 9916432 | tf_op jit(solution)/shard_map/all_gather | solution.py:195
  478.2 10.6 fusion.98
  488.9 8.7 multiply_reduce_fusion.2
  497.6 1.9 fusion.91
  499.5 3.2 fusion.74
  504.0 3.6 convolution_convert_fusion
  507.6 1.3 copy.53
  509.0 3.8 fusion.99
  512.8 9.1 fusion.51
  521.8 10.1 fusion.93
  531.9 4.2 fusion.92
  536.1 0.8 copy-done.4
  536.9 8.1 fusion.69
  545.8 11.5 fusion.65
  559.2 252.6 %reduce-scatter.24.cloned.1.call-done = f32[144,4304]{1,0:T(8,128)} async-done(((f32[1152,4304]{1,0:T(8,128)}), f32[144,4304]{1,0:T(8,128)}) %reduce-scatter.24.cloned.1.call-update) | async-done | bytes 2479120
  811.8 4.8 copy.64
  816.7 102.0 %reduce-scatter.20.cloned.1.call-done = f32[144,1152]{1,0:T(8,128)} async-done(((f32[1152,1152]{1,0:T(8,128)}), f32[144,1152]{1,0:T(8,128)}) %reduce-scatter.20.cloned.1.call-update) | async-done | bytes 663568 | tf_op jit(solution)/shard_map/reduce_scatter | solution.py:212
  918.8 272.1 %reduce-scatter.18.cloned.1.call-done = f32[144,3456]{1,0:T(8,128)} async-done(((f32[1152,3456]{1,0:T(8,128)}), f32[144,3456]{1,0:T(8,128)}) %reduce-scatter.18.cloned.1.call-update) | async-done | bytes 1990672 | tf_op jit(solution)/shard_map/reduce_scatter | solution.py:211
  1190.9 334.6 %reduce-scatter.22.cloned.1.call-done = f32[144,4304]{1,0:T(8,128)} async-done(((f32[1152,4304]{1,0:T(8,128)}), f32[144,4304]{1,0:T(8,128)}) %reduce-scatter.22.cloned.1.call-update) | async-done | bytes 2479120 | tf_op jit(solution)/shard_map/reduce_scatter | solution.py:213
  1525.5 103.3 %fusion.90 = (f32[48,3456]{1,0:T(8,128)}, f32[48,1152]{1,0:T(8,128)}, f32[40,4304]{1,0:T(8,128)}) fusion(f32[144,3456]{1,0:T(8,128)} %reduce-scatter.18.cloned.1.call-done, f32[144,1152]{1,0:T(8,128)} %reduce-scatter.20.cloned.1.call-done, f32[144,4304]{1,0:T(8,128)} %reduce-scatter.22.cloned.1.call-done), kind=kCustom, calls=%all-reduce-scatter.3 | all-reduce-scatter fusion | flops 1573378 | bytes 6707200
  1628.8 1.9 slice.58
  1630.7 2.6 collective-permute-start
  1633.3 8.0 fusion.61
  1641.3 0.8 stack.29
  1642.1 0.8 stack.30
  1642.9 0.7 stack.31
  1643.6 0.7 stack.32
  1645.8 1.1 copy.67
  1647.0 7.0 concatenate.5
  1654.0 2.0 dynamic-slice_bitcast_fusion.2
  1656.1 1.0 slice.60
  1657.1 8.6 collective-permute-start.2
  1666.8 5.1 concatenate.7
  1671.9 2.1 dynamic-slice_bitcast_fusion.1
  1674.9 4.3 dynamic-slice_bitcast_fusion
  1679.2 3.2 copy.57
  1682.5 9.5 fusion.23
  1692.0 6.7 collective-permute-start.1
  1698.7 1.3 fusion.71
  1700.0 39.0 %psum.7 = f32[4304]{0:T(1024)} all-reduce(f32[4304]{0:T(1024)S(1)} %copy-done.34), channel_id=1, replica_groups=mesh['rep'=4,'shard'=8] {'rep','shard'}, use_global_device_ids=true, to_apply=%region_30.0 | all-reduce | flops 4304 | bytes 34432 | tf_op jit(solution)/shard_map/psum | solution.py:209
  1739.0 0.9 copy.68
  1740.0 7.3 all-reduce.4
  1747.3 5.2 all-gather.5
  1753.5 9.9 all-gather.2
  1763.4 0.9 reshape.198
  1764.3 2.6 reshape.196
  1767.0 10.6 all-gather.24.cloned.1.call-done
  1777.5 2.9 reshape.200
  1780.5 26.0 %all-gather.26.cloned.1.call-done = f32[4,36,4304]{2,1,0:T(8,128)} async-done(((f32[1,36,4304]{2,1,0:T(8,128)}), f32[4,36,4304]{2,1,0:T(8,128)}) %all-gather.26.cloned.1.call-update) | async-done | bytes 2479120 | tf_op jit(solution)/shard_map/all_gather | solution.py:228
  1806.5 2.9 reshape.202
  (147 shorter events, 12.9 us)
Async XLA Ops:
  7.2 2.9 copy-start.39
  7.2 36.4 %copy-start.36 = (bf16[4304]{0:T(1024)(128)(2,1)S(1)}, bf16[4304]{0:T(1024)(128)(2,1)}, u32[]{:S(2)}) copy-start(bf16[4304]{0:T(1024)(128)(2,1)} %param.15) | copy-start | bytes 25828
  7.2 37.6 %copy-start.1 = (bf16[1,256,1152]{2,1,0:T(8,128)(2,1)S(1)}, bf16[1,256,1152]{2,1,0:T(8,128)(2,1)}, u32[]{:S(2)}) copy-start(bf16[1,256,1152]{2,1,0:T(8,128)(2,1)} %param.8) | copy-start | bytes 1769476
  7.2 125.0 %all-gather.14.cloned.1.call-start = ((), (), s32[]{:S(2)}) async-start(), calls=%async_computation.5 | async-start | bytes 8957952 | tf_op jit(solution)/shard_map/all_gather | solution.py:192
  7.9 179.6 %all-gather.16.cloned.1.call-start = ((), (), s32[]{:S(2)}) async-start(), calls=%async_computation.6 | async-start | bytes 2985984 | tf_op jit(solution)/shard_map/all_gather | solution.py:193
  8.7 324.5 %all-gather.18.cloned.1.call-start = ((), (), s32[]{:S(2)}) async-start(), calls=%async_computation.7 | async-start | bytes 11280384 | tf_op jit(solution)/shard_map/all_gather | solution.py:194
  9.4 468.8 %all-gather.20.cloned.1.call-start = ((), (), s32[]{:S(2)}) async-start(), calls=%async_computation.8 | async-start | bytes 11280384 | tf_op jit(solution)/shard_map/all_gather | solution.py:195
  10.0 801.8 %reduce-scatter.24.cloned.1.call-start = ((), (), s32[]{:S(2)}) async-start(), calls=%async_computation.15 | async-start | bytes 22560768
  44.8 93.4 %copy-start.20 = (f32[1152]{0:T(1024)}, f32[1152]{0:T(1024)S(1)}, u32[]{:S(2)}) copy-start(f32[1152]{0:T(1024)S(1)} %get-tuple-element.22) | copy-start | bytes 13828
  45.0 93.2 %copy-start.26 = (f32[256]{0:T(256)}, f32[256]{0:T(256)S(1)}, u32[]{:S(2)}) copy-start(f32[256]{0:T(256)S(1)} %broadcast_multiply_fusion.5) | copy-start | bytes 3076
  45.3 92.9 %copy-start.31 = (f32[256]{0:T(256)}, f32[256]{0:T(256)S(1)}, u32[]{:S(2)}) copy-start(f32[256]{0:T(256)S(1)} %add_rsqrt_fusion.1) | copy-start | bytes 3076
  138.7 2.1 copy-start.7
  139.0 1.0 copy-start.8
  139.2 1.5 copy-start.6
  140.0 2.0 copy-start
  140.0 3.0 copy-start.16
  140.8 2.3 copy-start.22
  142.0 45.6 %copy-start.38 = (f32[1152]{0:T(1024)S(1)}, f32[1152]{0:T(1024)}, u32[]{:S(2)}) copy-start(f32[1152]{0:T(1024)} %get-tuple-element.19) | copy-start | bytes 13828
  143.0 47.4 %copy-start.11 = (bf16[16,72,256]{2,1,0:T(8,128)(2,1)}, bf16[16,72,256]{2,1,0:T(8,128)(2,1)S(1)}, u32[]{:S(2)}) copy-start(bf16[16,72,256]{2,1,0:T(8,128)(2,1)S(1)} %fusion.50) | copy-start | bytes 1769476
  187.6 145.6 %copy-start.18 = (f32[1152]{0:T(1024)S(1)}, f32[1152]{0:T(1024)}, u32[]{:S(2)}) copy-start(f32[1152]{0:T(1024)} %get-tuple-element.18) | copy-start | bytes 13828
  187.6 145.6 %copy-start.35 = (f32[4304]{0:T(1024)S(1)}, f32[4304]{0:T(1024)}, u32[]{:S(2)}) copy-start(f32[4304]{0:T(1024)} %convert_element_type.84) | copy-start | bytes 51652
  190.5 298.4 %copy-start.24 = (f32[256]{0:T(256)}, f32[256]{0:T(256)S(1)}, u32[]{:S(2)}) copy-start(f32[256]{0:T(256)S(1)} %broadcast_multiply_fusion.4) | copy-start | bytes 3076
  190.8 298.1 %copy-start.29 = (f32[256]{0:T(256)}, f32[256]{0:T(256)S(1)}, u32[]{:S(2)}) copy-start(f32[256]{0:T(256)S(1)} %add_rsqrt_fusion) | copy-start | bytes 3076
  333.2 10.1 copy-start.3
  341.2 2.1 copy-start.2
  373.5 545.2 %reduce-scatter.20.cloned.1.call-start = ((), (), s32[]{:S(2)}) async-start(), calls=%async_computation.10 | async-start | bytes 5971968 | tf_op jit(solution)/shard_map/reduce_scatter | solution.py:212
  488.9 8.7 copy-start.9
  497.6 1.9 copy-start.12
  502.7 0.7 copy-start.17
  502.7 0.7 copy-start.23
  502.7 688.2 %reduce-scatter.18.cloned.1.call-start = ((), (), s32[]{:S(2)}) async-start(), calls=%async_computation.9 | async-start | bytes 17915904 | tf_op jit(solution)/shard_map/reduce_scatter | solution.py:211
  531.9 5.0 copy-start.14
  531.9 5.0 copy-start.15
  531.9 5.0 copy-start.21
  531.9 5.0 copy-start.27
  531.9 5.0 copy-start.32
  536.1 0.8 copy-start.4
  545.1 0.7 copy-start.19
  545.1 0.7 copy-start.25
  545.1 0.7 copy-start.30
  545.1 980.4 %reduce-scatter.22.cloned.1.call-start = ((), (), s32[]{:S(2)}) async-start(), calls=%async_computation.11 | async-start | bytes 22560768 | tf_op jit(solution)/shard_map/reduce_scatter | solution.py:213
  557.3 0.7 copy-start.40
  557.3 1117.6 %all-reduce.11.cloned.1.call-start = ((), (), s32[]{:S(2)}) async-start(), calls=%async_computation.17 | async-start | bytes 8814592
  816.7 816.6 %copy-start.5 = (bf16[1,256,16,72]{1,3,2,0:T(8,128)(2,1)S(1)}, bf16[1,256,16,72]{1,3,2,0:T(8,128)(2,1)}, u32[]{:S(2)}) copy-start(bf16[1,256,16,72]{1,3,2,0:T(8,128)(2,1)} %copy-done.4) | copy-start | bytes 1769476
  816.7 816.6 %copy-start.28 = (f32[256]{0:T(256)S(1)}, f32[256]{0:T(256)}, u32[]{:S(2)}) copy-start(f32[256]{0:T(256)} %copy-done.26) | copy-start | bytes 3076
  816.7 816.6 %copy-start.33 = (f32[256]{0:T(256)S(1)}, f32[256]{0:T(256)}, u32[]{:S(2)}) copy-start(f32[256]{0:T(256)} %copy-done.31) | copy-start | bytes 3076
  816.7 922.3 %reduce-scatter.26.cloned.1.call-start = ((), (), s32[]{:S(2)}) async-start(), calls=%async_computation.16 | async-start | bytes 663552
  1630.7 16.3 collective-permute-start
  1646.9 117.4 %all-gather.22.cloned.1.call-start = ((), (), s32[]{:S(2)}) async-start(), calls=%async_computation.12 | async-start | bytes 2764800 | tf_op jit(solution)/shard_map/all_gather | solution.py:225
  1656.0 121.5 %all-gather.24.cloned.1.call-start = ((), (), s32[]{:S(2)}) async-start(), calls=%async_computation.13 | async-start | bytes 3481600 | tf_op jit(solution)/shard_map/all_gather | solution.py:227
  1657.1 9.8 collective-permute-start.2
  1674.0 132.5 %all-gather.26.cloned.1.call-start = ((), (), s32[]{:S(2)}) async-start(), calls=%async_computation.14 | async-start | bytes 3481600 | tf_op jit(solution)/shard_map/all_gather | solution.py:228
  1679.2 3.2 copy-start.42
  1679.2 3.2 copy-start.41
  1679.2 3.3 copy-start.37
  1682.5 9.5 copy-start.10
  1682.5 16.2 copy-start.13
  1692.0 8.0 copy-start.34
  1692.0 61.2 %collective-permute-start.1 = (f32[36,1152]{1,0:T(8,128)S(1)}, f32[36,1152]{1,0:T(8,128)S(1)}, u32[]{:S(2)}, u32[]{:S(2)}) collective-permute-start(f32[36,1152]{1,0:T(8,128)S(1)} %slice.59), channel_id=1, source_target_pairs={{0,8},{8,16},{16,24},{1,9},{9,17},{17,25},{2,10},{10,18},{18,26},{... | collective-permute-start | bytes 497672
Sparse Core Ops, SparseCore 0:
  10.2 121.9 all-gather.13
  134.4 53.1 all-gather.15
  189.7 143.3 all-gather.17
  335.2 142.9 all-gather.19
  482.0 329.7 reduce-scatter.23
  815.2 103.4 reduce-scatter.19
  922.7 268.1 reduce-scatter.17
  1194.8 330.6 reduce-scatter.21
  1527.9 129.9 all-reduce.10
  1661.1 63.0 reduce-scatter.25
  1725.8 22.8 all-gather.21
  1750.1 27.4 all-gather.23
  1779.1 27.3 all-gather.25
where the time goes:
time: 1820 us
  waiting for transfers between devices  1380 us (76%)
  blocking collectives  198 us (11%)
  matrix products  118 us (6%)
  local copies, waits for them, and re-layouts  78.8 us (4%)
  starting transfers between devices  19.2 us (1%)
    reduce_scatter x1, waiting for transfers between devices, per_device(): lax.psum_scatter(terms[2], 'shard', scatter_dimension=0, tiled=True)  335 us
    reduce_scatter x1, waiting for transfers between devices, per_device(): lax.psum_scatter(terms[0], 'shard', scatter_dimension=0, tiled=True)  272 us
    unnamed x19, waiting for transfers between devices  256 us
    all_gather x1, waiting for transfers between devices, per_device(): lax.all_gather(w_up, 'shard', axis=0, tiled=True)  142 us
    unnamed x2, blocking collectives  111 us
    all_gather x1, waiting for transfers between devices, per_device(): lax.all_gather(w_down, 'shard', axis=0, tiled=True)  105 us
    reduce_scatter x1, waiting for transfers between devices, per_device(): lax.psum_scatter(terms[1], 'shard', scatter_dimension=0, tiled=True)  102 us
    all_gather x1, waiting for transfers between devices, per_device(): lax.all_gather(w_qkv, 'shard', axis=0, tiled=True)  86.9 us
  transfers between devices with their start and end apart: 16, of which 11 were waited for; matrix products, arithmetic and copies ran while one was open for 16% of the time, Pallas kernels for 0%

commit v1 on v0

v1 whole, which is shorter than its diff:
```python
import math

import jax
import jax.numpy as jnp
from jax import lax
from jax.sharding import PartitionSpec as P

HEAD_DIM = 72
EPSILON = 1e-06
GELU_COEF = 0.044715
ROOT_TWO_PI = math.sqrt(2.0 / math.pi)
F32 = jnp.float32
BF16 = jnp.bfloat16


def dot(a, b, ca, cb):
    return lax.dot_general(a, b, (((ca,), (cb,)), ((), ())), preferred_element_type=F32)


def batched(pattern, left_op, right_op):
    return jnp.einsum(pattern, left_op, right_op, preferred_element_type=F32)


def norm_rows(hidden):
    row_mean = jnp.mean(hidden, axis=-1, keepdims=True)
    centered = hidden - row_mean
    variance = jnp.mean(centered * centered, axis=-1, keepdims=True)
    inv_std = lax.rsqrt(variance + EPSILON)
    return (centered * inv_std, inv_std)


def norm_back(grad_normed, normed, inv_std):
    mean_grad = jnp.mean(grad_normed, axis=-1, keepdims=True)
    mean_proj = jnp.mean(grad_normed * normed, axis=-1, keepdims=True)
    return inv_std * (grad_normed - mean_grad - normed * mean_proj)


def gelu_parts(u):
    t = jnp.tanh(ROOT_TWO_PI * (u + GELU_COEF * u * u * u))
    act = 0.5 * u * (1.0 + t)
    der = 0.5 * (1.0 + t) + 0.5 * u * (1.0 - t * t) * ROOT_TWO_PI * (
        1.0 + 3.0 * GELU_COEF * u * u
    )
    return act, der


def gather_rep(a):
    return lax.all_gather(a, "rep", axis=0, tiled=True)


def scatter_rep(a):
    return lax.psum_scatter(a.astype(BF16), "rep", scatter_dimension=0, tiled=True).astype(F32)


def per_device(reps, images, cotangent, w_qkv, w_out, w_up, w_down, vectors, up_bias):
    r = lax.axis_index("rep")
    batch, seq, width = images.shape
    rows = w_qkv.shape[0]
    quarter = width // reps
    ffq = w_up.shape[1] // reps
    heads = quarter // HEAD_DIM

    def take(w, start, size):
        return lax.dynamic_slice_in_dim(w, start, size, 1)

    part = jnp.concatenate(
        [take(w_qkv, t * width + r * quarter, quarter) for t in range(3)], axis=1
    )
    mine_up = take(w_up, r * ffq, ffq)
    mine_down = take(w_down, r * ffq, ffq)
    wq = lax.all_gather(part, "shard", axis=0, tiled=True)
    wo = lax.all_gather(w_out, "shard", axis=0, tiled=True)
    wu = lax.all_gather(mine_up, "shard", axis=0, tiled=True)
    wd = lax.all_gather(mine_down, "shard", axis=0, tiled=True)
    params = lax.all_gather(vectors, "shard", axis=0, tiled=True).astype(F32)
    wo = lax.dynamic_slice_in_dim(wo, r * quarter, quarter, 0)
    bias_up = lax.dynamic_slice_in_dim(up_bias, r * ffq, ffq, 0).astype(F32)

    x = images.reshape(batch * seq, width).astype(F32)
    e = cotangent.reshape(batch * seq, width)
    e_all = gather_rep(e)
    n1, r1 = norm_rows(x)
    a1 = gather_rep((n1 * params[:, 0] + params[:, 1]).astype(BF16))
    proj = dot(a1, wq, 1, 0)
    bq = lax.dynamic_slice_in_dim(params[:, 2], r * quarter, quarter, 0)
    bv = lax.dynamic_slice_in_dim(params[:, 3], r * quarter, quarter, 0)
    group = reps * batch

    def split(t):
        return t.reshape(group, seq, heads, HEAD_DIM)

    q = split((proj[:, :quarter] + bq).astype(BF16))
    k = split(proj[:, quarter : 2 * quarter].astype(BF16))
    v = split((proj[:, 2 * quarter :] + bv).astype(BF16))
    scale = 1.0 / math.sqrt(HEAD_DIM)
    s = batched("bqhd,bkhd->bhqk", q, k) * scale
    top = jnp.max(s, axis=-1, keepdims=True)
    ex = jnp.exp(s - top)
    total = jnp.sum(ex, axis=-1, keepdims=True)
    probs = ex / total
    probs_bf = probs.astype(BF16)
    o = batched("bhqk,bkhd->bqhd", probs_bf, v).reshape(group * seq, quarter).astype(BF16)
    m = x + scatter_rep(dot(o, wo, 1, 0)) + params[:, 4]
    n2, r2 = norm_rows(m)
    a2 = gather_rep((n2 * params[:, 5] + params[:, 6]).astype(BF16))
    act, der = gelu_parts(dot(a2, wu, 1, 0) + bias_up)
    act = act.astype(BF16)
    final = m + scatter_rep(dot(act, wd, 1, 1)) + params[:, 7]
    outputs = final.astype(BF16).reshape(batch, seq, width)

    def reduce_rows(term):
        return lax.psum_scatter(term.astype(BF16), "shard", scatter_dimension=0, tiled=True)

    ef = e.astype(F32)
    g_down = reduce_rows(dot(e_all, act, 0, 0))
    du = dot(e_all, wd, 1, 0) * der
    upb = jnp.sum(du, axis=0)
    dub = du.astype(BF16)
    g_up = reduce_rows(dot(a2, dub, 0, 0))
    da2 = scatter_rep(dot(dub, wu, 1, 1))
    dm = ef + norm_back(da2 * params[:, 5], n2, r2)
    dmb = gather_rep(dm.astype(BF16))
    do = dot(dmb, wo, 1, 1).astype(BF16)
    out_term = dot(o, dmb, 0, 0).astype(BF16)
    out_term = lax.dynamic_update_slice_in_dim(
        jnp.zeros((width, width), BF16), out_term, r * quarter, 0
    )
    g_out = lax.psum_scatter(out_term, "shard", scatter_dimension=0, tiled=True)
    do = split(do)
    dv = batched("bhqk,bqhd->bkhd", probs_bf, do)
    dpr = batched("bqhd,bkhd->bhqk", do, v)
    delta = jnp.sum(probs * dpr, axis=-1, keepdims=True)
    ds = (probs * (dpr - delta) * scale).astype(BF16)
    dq = batched("bhqk,bkhd->bqhd", ds, k)
    dk = batched("bhqk,bqhd->bkhd", ds, q)
    dp = jnp.concatenate([t.reshape(group * seq, quarter) for t in (dq, dk, dv)], axis=1)
    col = jnp.sum(dp, axis=0)
    dp = dp.astype(BF16)
    g_qkv = reduce_rows(dot(a1, dp, 0, 0))
    da1 = scatter_rep(dot(dp, wq, 1, 1))
    input_grad = dm + norm_back(da1 * params[:, 0], n1, r1)
    input_grad = input_grad.astype(BF16).reshape(batch, seq, width)

    def place(piece):
        return lax.dynamic_update_slice_in_dim(jnp.zeros((width,), F32), piece, r * quarter, 0)

    vec = jnp.stack(
        [
            jnp.sum(da1 * n1, axis=0),
            jnp.sum(da1, axis=0),
            place(col[:quarter]),
            place(col[2 * quarter :]),
            jnp.sum(dm, axis=0),
            jnp.sum(da2 * n2, axis=0),
            jnp.sum(da2, axis=0),
            jnp.sum(ef, axis=0),
        ],
        axis=1,
    )
    vec = lax.psum(lax.psum_scatter(vec, "shard", scatter_dimension=0, tiled=True), "rep")
    upb = lax.all_gather(lax.psum(upb, "shard"), "rep", axis=0, tiled=True)

    def columns(g):
        return lax.all_gather(g, "rep", axis=0).transpose(1, 0, 2).astype(F32)

    g_down = columns(g_down).reshape(rows, -1)
    g_up = columns(g_up).reshape(rows, -1)
    g_qkv = columns(g_qkv).reshape(rows, reps, 3, quarter).transpose(0, 2, 1, 3).reshape(rows, -1)
    g_out = lax.psum(g_out, "rep").astype(F32)
    return (outputs, input_grad, g_qkv, g_out, g_up, g_down, vec, upb)


def solution(mesh):
    reps = mesh.shape["rep"]
    token = P(("rep", "shard"), None, None)
    row = P("shard", None)

    def body(*args):
        return per_device(reps, *args)

    return jax.shard_map(
        body,
        mesh=mesh,
        in_specs=(token, token, row, row, row, row, row, P()),
        out_specs=(token, token, row, row, row, row, row, P()),
        check_vma=False,
    )
```

time: 1820 us -> 939 us (0.52)
  waiting for transfers between devices: 1380 us -> 645 us
  blocking collectives: 198 us -> 75.6 us
  other arithmetic: 6.03 us -> 30.9 us
  matrix products: 118 us -> 96.5 us
    reduce_scatter x3 -> x8, waiting for transfers between devices: 709 us -> 303 us  [the longest x3 158 us: reduce_rows(): lax.psum_scatter(term.astype(BF16), 'shard', scatter_dimension=0, tiled=T...]
    unnamed x19 -> x21, waiting for transfers between devices: 256 us -> 64.9 us
    all_gather x7 -> x10, waiting for transfers between devices: 415 us -> 256 us  [the longest x4 92.5 us: gather_rep(): return lax.all_gather(a, 'rep', axis=0, tiled=True)]
    unnamed x2 -> x0, blocking collectives: 111 us -> none
    unnamed x108 -> x58, local copies, waits for them, and re-layouts: 71.5 us -> 18.5 us
    reshape x0 -> x11, local copies, waits for them, and re-layouts: none -> 32.9 us  [the longest x3 14.5 us: per_device(): columns(g_qkv).reshape(rows, reps, 3, quarter).transpose(0, 2, 1, 3)]
    dot_general x18, matrix products: 118 us -> 96.5 us  [the longest x12 71 us: dot(): lax.dot_general(a, b, (((ca,), (cb,)), ((), ())), preferred_element_type=...]
    psum x0 -> x1, waiting for transfers between devices: none -> 21.2 us  [per_device(): g_out = lax.psum(g_out, 'rep').astype(F32)]
  transfers between devices with their start and end apart: 16 -> 20, of which waited for: 11 -> 18; matrix products, arithmetic and copies ran while one was open for 16% -> 17% of each run, Pallas kernels for 0% -> 0%
where the time goes in v1:
time: 939 us; the launch traced here: 930 us
  waiting for transfers between devices  645 us (69%)
  matrix products  96.5 us (10%)
  blocking collectives  75.6 us (8%)
  local copies, waits for them, and re-layouts  63.5 us (7%)
  other arithmetic  30.9 us (3%)
  between operations  15.9 us (2%)
    reduce_scatter x3, waiting for transfers between devices, reduce_rows(): lax.psum_scatter(term.astype(BF16), 'shard', scatter_dimension=0, tiled=T...  158 us
    all_gather x4, waiting for transfers between devices, gather_rep(): return lax.all_gather(a, 'rep', axis=0, tiled=True)  92.5 us
    reduce_scatter x4, waiting for transfers between devices, scatter_rep(): lax.psum_scatter(a.astype(BF16), 'rep', scatter_dimension=0, tiled=True)  73.1 us
    reduce_scatter x1, waiting for transfers between devices, per_device(): g_out = lax.psum_scatter(out_term, 'shard', scatter_dimension=0, tiled=True)  72.2 us
    dot_general x12, matrix products, dot(): lax.dot_general(a, b, (((ca,), (cb,)), ((), ())), preferred_element_type=...  71 us
    unnamed x21, waiting for transfers between devices  64.9 us
    all_gather x1, waiting for transfers between devices, per_device(): wd = lax.all_gather(mine_down, 'shard', axis=0, tiled=True)  57.8 us
    all_gather x1, waiting for transfers between devices, per_device(): wu = lax.all_gather(mine_up, 'shard', axis=0, tiled=True)  49.8 us
  transfers between devices with their start and end apart: 20, of which 18 were waited for; matrix products, arithmetic and copies ran while one was open for 17% of the time, Pallas kernels for 0%

profile of v1, /device:TPU:0, one launch (start us, length us, event | category | flops | bytes accessed | tf_op | source)
XLA Modules:
  0.0 929.8 jit_solution(6168868636376953412)
XLA Ops:
  9.5 32.7 %all-gather.4 = bf16[8,144,8]{1,2,0:T(8,128)(2,1)S(1)} all-gather(bf16[1,144,8]{1,2,0:T(8,128)(2,1)} %bitcast.161), channel_id=1, replica_groups=mesh['rep'=4,'shard'=8] {'shard'}, dimensions={0}, use_global_device_ids=true | all-gather | bytes 20736 | tf_op jit(solution)/shard_map/all_gather | solution.py:75
  46.0 16.3 %all-gather.18.cloned.1.call-done = bf16[1152,864]{1,0:T(8,128)(2,1)} async-done(((bf16[144,864]{1,0:T(8,128)(2,1)}), bf16[1152,864]{1,0:T(8,128)(2,1)}) %all-gather.18.cloned.1.call-update) | async-done | bytes 1990672 | tf_op jit(solution)/shard_map/all_gather | solution.py:71
  62.3 24.8 %all-gather.16.cloned.1.call-done = bf16[1024,1152]{1,0:T(8,128)(2,1)} async-done(((bf16[256,1152]{1,0:T(8,128)(2,1)}), bf16[1024,1152]{1,0:T(8,128)(2,1)}) %all-gather.16.cloned.1.call-update) | async-done | bytes 2359312 | tf_op jit(solution)/shard_map/all_gather | solution.py:48
  87.1 4.8 fusion.99
  94.7 2.0 reshape.132
  96.7 2.0 fusion.79
  98.7 3.2 fusion.97
  102.5 1.5 copy-done.8
  104.5 39.8 %all-gather.20.cloned.1.call-done = bf16[1152,1152]{1,0:T(8,128)(2,1)} async-done(((bf16[144,1152]{1,0:T(8,128)(2,1)}), bf16[1152,1152]{1,0:T(8,128)(2,1)}) %all-gather.20.cloned.1.call-update) | async-done | bytes 2654224 | tf_op jit(solution)/shard_map/all_gather | solution.py:72
  144.3 4.0 convolution_convert_fusion.3
  149.4 30.5 %reduce-scatter.14.cloned.1.call-done = bf16[256,1152]{1,0:T(8,128)(2,1)} async-done(((bf16[1024,1152]{1,0:T(8,128)(2,1)}), bf16[256,1152]{1,0:T(8,128)(2,1)}) %reduce-scatter.14.cloned.1.call-update) | async-done | bytes 589840 | tf_op jit(solution)/shard_map/reduce_scatter | solution.py:52
  184.7 1.9 constant_dynamic-slice_fusion
  187.7 49.8 %all-gather.24.cloned.1.call-done = bf16[1152,1076]{1,0:T(8,128)(2,1)} async-done(((bf16[144,1076]{1,0:T(8,128)(2,1)}), bf16[1152,1076]{1,0:T(8,128)(2,1)}) %all-gather.24.cloned.1.call-update) | async-done | bytes 2479120 | tf_op jit(solution)/shard_map/all_gather | solution.py:73
  237.5 24.6 %all-gather.22.cloned.1.call-done = bf16[1024,1152]{1,0:T(8,128)(2,1)} async-done(((bf16[256,1152]{1,0:T(8,128)(2,1)}), bf16[1024,1152]{1,0:T(8,128)(2,1)}) %all-gather.22.cloned.1.call-update) | async-done | bytes 2359312 | tf_op jit(solution)/shard_map/all_gather | solution.py:48
  262.1 7.5 convolution_add_fusion
  269.7 18.1 %all-gather.30.cloned.1.call-done = bf16[1,1024,1152]{2,1,0:T(8,128)(2,1)} async-done(((bf16[1,256,1152]{2,1,0:T(8,128)(2,1)}), bf16[1,1024,1152]{2,1,0:T(8,128)(2,1)}) %all-gather.30.cloned.1.call-update) | async-done | bytes 2359312 | tf_op jit(solution)/shard_map/all_gather | solution.py:48
  287.7 57.8 %all-gather.26.cloned.1.call-done = bf16[1152,1076]{1,0:T(8,128)(2,1)} async-done(((bf16[144,1076]{1,0:T(8,128)(2,1)}), bf16[1152,1076]{1,0:T(8,128)(2,1)}) %all-gather.26.cloned.1.call-update) | async-done | bytes 2479120 | tf_op jit(solution)/shard_map/all_gather | solution.py:74
  345.5 8.8 fusion.98
  355.7 5.0 convolution_convert_fusion.4
  361.1 8.8 convolution_convert_fusion.5
  370.0 7.2 convolution_convert_fusion.1
  377.3 8.3 fusion.2
  385.7 5.2 copy.96
  392.2 1.8 fusion.59
  394.0 33.4 %reduce-scatter.16.cloned.1.call-done = bf16[256,1152]{1,0:T(8,128)(2,1)} async-done(((bf16[1024,1152]{1,0:T(8,128)(2,1)}), bf16[256,1152]{1,0:T(8,128)(2,1)}) %reduce-scatter.16.cloned.1.call-update) | async-done | bytes 589840 | tf_op jit(solution)/shard_map/reduce_scatter | solution.py:52
  427.4 2.8 fusion.93
  431.2 71.1 %reduce-scatter.26.cloned.1.call-done = bf16[144,1076]{1,0:T(8,128)(2,1)} async-done(((bf16[1152,1076]{1,0:T(8,128)(2,1)}), bf16[144,1076]{1,0:T(8,128)(2,1)}) %reduce-scatter.26.cloned.1.call-update) | async-done | bytes 309904 | tf_op jit(solution)/shard_map/reduce_scatter | solution.py:112
  502.4 74.0 %reduce-scatter.28.cloned.1.call-done = bf16[144,1076]{1,0:T(8,128)(2,1)} async-done(((bf16[1152,1076]{1,0:T(8,128)(2,1)}), bf16[144,1076]{1,0:T(8,128)(2,1)}) %reduce-scatter.28.cloned.1.call-update) | async-done | bytes 309904 | tf_op jit(solution)/shard_map/reduce_scatter | solution.py:112
  576.6 25.0 %all-gather.28.cloned.1.call-done = bf16[1024,1152]{1,0:T(8,128)(2,1)} async-done(((bf16[256,1152]{1,0:T(8,128)(2,1)}), bf16[1024,1152]{1,0:T(8,128)(2,1)}) %all-gather.28.cloned.1.call-update) | async-done | bytes 2359312 | tf_op jit(solution)/shard_map/all_gather | solution.py:48
  601.6 3.6 convolution_convert_fusion.8
  605.1 1.7 reshape.137
  606.9 3.2 convolution_bitcast_fusion
  612.2 2.7 fusion.74
  614.9 8.4 fusion.42
  623.2 2.1 copy.84
  626.6 8.7 fusion.39
  635.3 2.0 copy.81
  639.1 1.7 copy-done.4
  640.9 4.0 convolution_convert_fusion.6
  645.2 7.0 convolution_convert_fusion.2
  652.3 1.7 broadcast_in_dim.2
  655.1 1.8 fusion.15
  658.7 21.7 %psum.23 = f32[1076]{0:T(1024)S(1)} all-reduce(f32[1076]{0:T(1024)S(1)} %get-tuple-element.44), channel_id=1, replica_groups=mesh['rep'=4,'shard'=8] {'shard'}, use_global_device_ids=true, to_apply=%region_30.0 | all-reduce | flops 1076 | bytes 8608 | tf_op jit(solution)/shard_map/psum | solution.py:161
  680.8 1.5 convert_bitcast_fusion.1
  682.3 2.6 copy.89
  684.9 3.9 reshape.152
  688.9 1.5 convert_bitcast_fusion
  690.4 2.6 copy.91
  693.0 3.9 reshape.154
  696.9 2.4 reduce_sum.174
  699.8 12.9 %reduce-scatter.22.cloned.1.call-done = bf16[144,864]{1,0:T(8,128)(2,1)} async-done(((bf16[1152,864]{1,0:T(8,128)(2,1)}), bf16[144,864]{1,0:T(8,128)(2,1)}) %reduce-scatter.22.cloned.1.call-update) | async-done | bytes 248848 | tf_op jit(solution)/shard_map/reduce_scatter | solution.py:112
  712.7 10.4 %all-gather.1 = bf16[576,864]{1,0:T(8,128)(2,1)S(1)} all-gather(bf16[144,864]{1,0:T(8,128)(2,1)} %reduce-scatter.22.cloned.1.call-done), channel_id=3, replica_groups=mesh['rep'=4,'shard'=8] {'rep'}, dimensions={0}, use_global_device_ids=true | all-gather | bytes 1244160 | tf_op jit(solution)/shard_map/all_gather | solution.py:164
  723.1 1.5 convert_bitcast_fusion.2
  724.5 5.2 reshape.159
  729.8 5.7 copy.88
  735.4 3.6 reshape.150
  739.0 7.9 reduce-scatter.20.cloned.1.call-done
  746.9 1.7 fusion.60
  749.8 72.2 %reduce-scatter.24.cloned.1.call-done = bf16[144,1152]{1,0:T(8,128)(2,1)} async-done(((bf16[1152,1152]{1,0:T(8,128)(2,1)}), bf16[144,1152]{1,0:T(8,128)(2,1)}) %reduce-scatter.24.cloned.1.call-update) | async-done | bytes 331792 | tf_op jit(solution)/shard_map/reduce_scatter | solution.py:128
  822.1 2.4 fusion.70
  824.5 63.2 %reduce-scatter.30.cloned.1.call-done = f32[144,8]{1,0:T(8,128)} async-done(((f32[1152,8]{1,0:T(8,128)}), f32[144,8]{1,0:T(8,128)}) %reduce-scatter.30.cloned.1.call-update) | async-done | bytes 4624
  888.6 10.9 %all-reduce.1 = (f32[144,8]{0,1:T(8,128)}, f32[4304]{0:T(1024)}) all-reduce(f32[144,8]{0,1:T(8,128)S(1)} %copy.99, f32[4304]{0:T(1024)S(1)} %dynamic-update-slice), channel_id=1, replica_groups=mesh['rep'=4,'shard'=8] {'rep'}, use_global_device_ids=true, to_apply=%region_28.0 | all-reduce | flops 5456 | bytes 43648 | tf_op jit(solution)/shard_map/psum | solution.py:160
  899.5 21.2 %all-reduce.4.cloned.1.call-done = bf16[144,1152]{1,0:T(8,128)(2,1)} async-done(((bf16[144,1152]{1,0:T(8,128)(2,1)}), bf16[144,1152]{1,0:T(8,128)(2,1)}) %all-reduce.4.cloned.1.call-update) | async-done | bytes 331792 | tf_op jit(solution)/shard_map/psum | solution.py:169
  920.7 1.9 convert_element_type.150
  (144 shorter events, 31.7 us)
Async XLA Ops:
  7.2 141.2 %copy-start = (bf16[144,4304]{1,0:T(8,128)(2,1)S(1)}, bf16[144,4304]{1,0:T(8,128)(2,1)}, u32[]{:S(2)}) copy-start(bf16[144,4304]{1,0:T(8,128)(2,1)} %param.12) | copy-start | bytes 3718660
  7.2 36.4 %copy-start.2 = (bf16[1,256,1152]{2,1,0:T(8,128)(2,1)S(1)}, bf16[1,256,1152]{2,1,0:T(8,128)(2,1)}, u32[]{:S(2)}) copy-start(bf16[1,256,1152]{2,1,0:T(8,128)(2,1)} %param.8) | copy-start | bytes 1769476
  7.2 55.1 %all-gather.18.cloned.1.call-start = ((), (), s32[]{:S(2)}) async-start(), calls=%async_computation.10 | async-start | bytes 2322432 | tf_op jit(solution)/shard_map/all_gather | solution.py:71
  9.5 77.6 %all-gather.16.cloned.1.call-start = ((), (), s32[]{:S(2)}) async-start(), calls=%async_computation.9 | async-start | bytes 2949120 | tf_op jit(solution)/shard_map/all_gather | solution.py:48
  45.1 99.2 %all-gather.20.cloned.1.call-start = ((), (), s32[]{:S(2)}) async-start(), calls=%async_computation.11 | async-start | bytes 2985984 | tf_op jit(solution)/shard_map/all_gather | solution.py:72
  45.8 134.0 %reduce-scatter.14.cloned.1.call-start = ((), (), s32[]{:S(2)}) async-start(), calls=%async_computation.12 | async-start | bytes 2949120 | tf_op jit(solution)/shard_map/reduce_scatter | solution.py:52
  94.7 4.0 copy-start.9
  96.7 5.3 copy-start.12
  102.0 2.0 copy-start.8
  104.5 43.8 %copy-start.16 = (bf16[36,8,4,256]{3,1,2,0:T(8,128)(2,1)}, bf16[36,8,4,256]{3,1,2,0:T(8,128)(2,1)S(1)}, u32[]{:S(2)}) copy-start(bf16[36,8,4,256]{3,1,2,0:T(8,128)(2,1)S(1)} %copy.100) | copy-start | bytes 1769476
  148.3 89.1 %all-gather.24.cloned.1.call-start = ((), (), s32[]{:S(2)}) async-start(), calls=%async_computation.14 | async-start | bytes 2985984 | tf_op jit(solution)/shard_map/all_gather | solution.py:73
  149.3 112.8 %all-gather.22.cloned.1.call-start = ((), (), s32[]{:S(2)}) async-start(), calls=%async_computation.13 | async-start | bytes 2949120 | tf_op jit(solution)/shard_map/all_gather | solution.py:48
  179.9 2.9 copy-start.3
  183.9 103.8 %all-gather.30.cloned.1.call-start = ((), (), s32[]{:S(2)}) async-start(), calls=%async_computation.24 | async-start | bytes 2949120 | tf_op jit(solution)/shard_map/all_gather | solution.py:48
  184.7 160.8 %all-gather.26.cloned.1.call-start = ((), (), s32[]{:S(2)}) async-start(), calls=%async_computation.15 | async-start | bytes 2985984 | tf_op jit(solution)/shard_map/all_gather | solution.py:74
  186.7 205.5 %reduce-scatter.18.cloned.1.call-start = ((), (), s32[]{:S(2)}) async-start(), calls=%async_computation.17 | async-start | bytes 2949120 | tf_op jit(solution)/shard_map/reduce_scatter | solution.py:52
  345.5 10.2 %copy-start.18 = (bf16[1152,1076]{1,0:T(8,128)(2,1)S(1)}, bf16[1152,1076]{1,0:T(8,128)(2,1)}, u32[]{:S(2)}) copy-start(bf16[1152,1076]{1,0:T(8,128)(2,1)} %all-gather.24.cloned.1.call-done) | copy-start | bytes 7437316
  354.3 1.4 copy-start.22
  360.7 66.7 %reduce-scatter.16.cloned.1.call-start = ((), (), s32[]{:S(2)}) async-start(), calls=%async_computation.16 | async-start | bytes 2949120 | tf_op jit(solution)/shard_map/reduce_scatter | solution.py:52
  370.0 132.3 %reduce-scatter.26.cloned.1.call-start = ((), (), s32[]{:S(2)}) async-start(), calls=%async_computation.23 | async-start | bytes 2985984 | tf_op jit(solution)/shard_map/reduce_scatter | solution.py:112
  377.3 199.1 %reduce-scatter.28.cloned.1.call-start = ((), (), s32[]{:S(2)}) async-start(), calls=%async_computation.27 | async-start | bytes 2985984 | tf_op jit(solution)/shard_map/reduce_scatter | solution.py:112
  390.9 36.5 %copy-start.5 = (bf16[1,256,1152]{2,1,0:T(8,128)(2,1)S(1)}, bf16[1,256,1152]{2,1,0:T(8,128)(2,1)}, u32[]{:S(2)}) copy-start(bf16[1,256,1152]{2,1,0:T(8,128)(2,1)} %param.9) | copy-start | bytes 1769476
  390.9 210.6 %all-gather.28.cloned.1.call-start = ((), (), s32[]{:S(2)}) async-start(), calls=%async_computation.18 | async-start | bytes 2949120 | tf_op jit(solution)/shard_map/all_gather | solution.py:48
  431.2 249.7 %all-gather.32.cloned.1.call-start = ((), (), s32[]{:S(2)}) async-start(), calls=%async_computation.25 | async-start | bytes 1658880 | tf_op jit(solution)/shard_map/all_gather | solution.py:164
  502.3 186.5 %all-gather.34.cloned.1.call-start = ((), (), s32[]{:S(2)}) async-start(), calls=%async_computation.26 | async-start | bytes 1658880 | tf_op jit(solution)/shard_map/all_gather | solution.py:164
  576.4 136.3 %reduce-scatter.22.cloned.1.call-start = ((), (), s32[]{:S(2)}) async-start(), calls=%async_computation.20 | async-start | bytes 2322432 | tf_op jit(solution)/shard_map/reduce_scatter | solution.py:112
  606.9 3.2 copy-start.14
  610.1 2.0 copy-start.13
  610.9 1.3 copy-start.15
  612.2 2.7 copy-start.11
  623.2 3.3 copy-start.10
  637.3 1.3 copy-start.7
  637.6 1.4 copy-start.6
  638.6 2.3 copy-start.19
  639.1 1.8 copy-start.4
  644.9 102.0 %reduce-scatter.20.cloned.1.call-start = ((), (), s32[]{:S(2)}) async-start(), calls=%async_computation.19 | async-start | bytes 2949120 | tf_op jit(solution)/shard_map/reduce_scatter | solution.py:52
  652.2 1.8 copy-start.17
  652.2 169.8 %reduce-scatter.24.cloned.1.call-start = ((), (), s32[]{:S(2)}) async-start(), calls=%async_computation.21 | async-start | bytes 2985984 | tf_op jit(solution)/shard_map/reduce_scatter | solution.py:128
  652.3 2.8 copy-start.20
  656.8 0.7 copy-start.21
  656.9 230.8 %reduce-scatter.30.cloned.1.call-start = ((), (), s32[]{:S(2)}) async-start(), calls=%async_computation.28 | async-start | bytes 663552
  749.7 172.8 %copy-start.1 = (bf16[144,4304]{1,0:T(8,128)(2,1)S(1)}, bf16[144,4304]{1,0:T(8,128)(2,1)}, u32[]{:S(2)}) copy-start(bf16[144,4304]{1,0:T(8,128)(2,1)} %param.12) | copy-start | bytes 3718660
  749.8 170.9 %all-reduce.4.cloned.1.call-start = ((), (), s32[]{:S(2)}) async-start(), calls=%async_computation.22 | async-start | bytes 663552 | tf_op jit(solution)/shard_map/psum | solution.py:169
Sparse Core Ops, SparseCore 0:
  10.8 51.4 all-gather.17
  64.4 22.6 all-gather.15
  89.3 54.9 all-gather.19
  148.4 31.3 reduce-scatter.13
  182.5 54.9 all-gather.23
  239.5 22.6 all-gather.21
  263.7 24.0 all-gather.29
  290.5 54.9 all-gather.25
  360.8 31.3 reduce-scatter.17
  394.6 32.8 reduce-scatter.15
  431.1 71.1 reduce-scatter.25
  505.8 70.4 reduce-scatter.27
  578.5 23.0 all-gather.27
  603.0 18.2 all-gather.31
  622.7 18.2 all-gather.33
  645.0 67.6 reduce-scatter.21
  715.1 31.7 reduce-scatter.19
  750.4 71.6 reduce-scatter.23
  825.9 61.6 reduce-scatter.29
  889.9 30.7 all-reduce.3

commit v2 on v1

v2 whole, which is shorter than its diff:
```python
import functools
import math

import jax
import jax.numpy as jnp
from jax import lax
from jax.experimental import pallas as pl
from jax.experimental.pallas import tpu as pltpu
from jax.sharding import PartitionSpec as P

HEAD_DIM = 72
EPSILON = 1e-06
GELU_COEF = 0.044715
ROOT_TWO_PI = math.sqrt(2.0 / math.pi)
SCALE = 1.0 / math.sqrt(HEAD_DIM)
F32 = jnp.float32
BF16 = jnp.bfloat16
RING = 8
HOPS = RING - 1


def dot(a, b, ca=1, cb=0):
    return lax.dot_general(a, b, (((ca,), (cb,)), ((), ())), preferred_element_type=F32)


def ring_row(pos):
    return 2 * pos + (pos // 4) * (15 - 4 * pos)


def mod8(v):
    return lax.rem(v + 4 * RING, RING)


def rows16(start, size):
    return pl.ds(pl.multiple_of(start, 16), size)


def normed(x):
    mean = jnp.mean(x, axis=-1, keepdims=True)
    cen = x - mean
    inv = lax.rsqrt(jnp.mean(cen * cen, axis=-1, keepdims=True) + EPSILON)
    return cen * inv, inv


def norm_back(dn, n, inv):
    a = jnp.mean(dn, axis=-1, keepdims=True)
    b = jnp.mean(dn * n, axis=-1, keepdims=True)
    return inv * (dn - a - n * b)


SCRATCH = dict(
    wb=lambda c: pltpu.VMEM((3, c.d, c.c), BF16),
    wo4=lambda c: pltpu.VMEM((4, c.q, c.qp), BF16),
    wo=lambda c: pltpu.VMEM((c.q, c.d), BF16),
    xa=lambda c: pltpu.VMEM((4, c.t, c.c), BF16),
    ea=lambda c: pltpu.VMEM((4, c.t, c.d), BF16),
    a1=lambda c: pltpu.VMEM((4, c.t, c.d), BF16),
    a2=lambda c: pltpu.VMEM((4, c.t, c.d), BF16),
    dmb=lambda c: pltpu.VMEM((4, c.t, c.d), BF16),
    pq=lambda c: pltpu.VMEM((4, c.t, c.c), BF16),
    oq=lambda c: pltpu.VMEM((4, c.t, c.qp), BF16),
    lse=lambda c: pltpu.VMEM((4, c.t, 128), F32),
    act=lambda c: pltpu.VMEM((4, c.t, c.c), BF16),
    der=lambda c: pltpu.VMEM((4, c.t, c.c), BF16),
    mid=lambda c: pltpu.VMEM((c.t, c.d), F32),
    dm=lambda c: pltpu.VMEM((c.t, c.d), F32),
    do=lambda c: pltpu.VMEM((4, c.t, c.qp), BF16),
    part=lambda c: pltpu.VMEM((4, c.t, c.d), BF16),
    xs=lambda c: pltpu.VMEM((c.t, c.d), BF16),
    cr=lambda c: pltpu.VMEM((2, 2, c.t, c.d), BF16),
    xr=lambda c: pltpu.VMEM((2, c.t, c.d), BF16),
    gd=lambda c: pltpu.VMEM((c.d, c.c), BF16),
    slot=lambda c: pltpu.VMEM((3, HOPS, c.b, c.c), BF16),
    fin=lambda c: pltpu.VMEM((3, 4, c.b, c.c), BF16),
    ogs=lambda c: pltpu.VMEM((4, c.q, c.qp), BF16),
    vb=lambda c: pltpu.VMEM((RING, c.b, 128), BF16),
    vt=lambda c: pltpu.VMEM((16, c.d), F32),
    vg=lambda c: pltpu.VMEM((RING, 8, c.d), F32),
    vf=lambda c: pltpu.VMEM((4, 8, c.d), F32),
    ag_s=lambda c: pltpu.SemaphoreType.DMA((3, 2, 2, HOPS)),
    ag_r=lambda c: pltpu.SemaphoreType.DMA((3, 2, 2, HOPS)),
    rs_s=lambda c: pltpu.SemaphoreType.DMA((3, 2, 2, HOPS)),
    rs_r=lambda c: pltpu.SemaphoreType.DMA((3, 2, 2, HOPS)),
    sm_s=lambda c: pltpu.SemaphoreType.DMA((2, 2, 4)),
    sm_r=lambda c: pltpu.SemaphoreType.DMA((2, 2, 4)),
    ex_s=lambda c: pltpu.SemaphoreType.DMA((8, 3)),
    ex_r=lambda c: pltpu.SemaphoreType.DMA((8, 3)),
    sum_s=lambda c: pltpu.SemaphoreType.DMA((4, 3)),
    sum_r=lambda c: pltpu.SemaphoreType.DMA((4, 3)),
    aa_s=lambda c: pltpu.SemaphoreType.DMA((2, 3)),
    aa_r=lambda c: pltpu.SemaphoreType.DMA((2, 3)),
    out_s=lambda c: pltpu.SemaphoreType.DMA((6,)),
)


class Sizes:
    def __init__(self, d, t, c, b, sub):
        self.d, self.t, self.c, self.b, self.sub = d, t, c, b, sub
        self.q = d // 4
        self.qp = -(-self.q // 128) * 128
        self.heads = self.q // HEAD_DIM


def kernel(c, w_ref, x_ref, e_ref, v_ref, ub_ref, out_ref, ing_ref, g0_ref, g1_ref, g2_ref, vo_ref, *refs):
    z = type("Refs", (), dict(zip(SCRATCH, refs)))
    d, t, nb, q, heads = c.d, c.t, c.b, c.q, c.heads
    r = lax.axis_index("rep")
    shard = lax.axis_index("shard")
    row, sub = shard // c.sub, lax.rem(shard, c.sub)
    za, yb = row // 2, lax.rem(row, 2)
    pos = za + yb * (7 - 2 * za)

    def ring_dev(p):
        return (r, ring_row(mod8(p)) * c.sub + sub)

    ahead = (ring_dev(pos + 1), ring_dev(pos - 1))
    core = r + 1 - 2 * lax.rem(r, 2)
    cross = lax.rem(r + 2, 4)
    diag = lax.rem(core + 2, 4)
    core_dev, cross_dev, diag_dev = (core, shard), (cross, shard), (diag, shard)

    pending = {}

    def rcopy(src, dst, ss, rs, dev):
        return pltpu.make_async_remote_copy(
            src_ref=src, dst_ref=dst, send_sem=ss, recv_sem=rs,
            device_id=dev, device_id_type=pl.DeviceIdType.MESH,
        )

    def send(src, dst, ss, rs, dev):
        cp = rcopy(src, dst, ss, rs, dev)
        cp.start()
        pending[id(cp)] = cp
        return cp

    def settle(cp):
        cp.wait_send()
        del pending[id(cp)]

    barrier = pltpu.get_barrier_semaphore()
    peers = (*ahead, core_dev, cross_dev, diag_dev)
    for dev in peers:
        pl.semaphore_signal(barrier, inc=1, device_id=dev, device_id_type=pl.DeviceIdType.MESH)
    pl.semaphore_wait(barrier, len(peers))

    half = (nb // 2 + 15) // 16 * 16
    bands = ((0, half), (half, nb - half))
    tiles = c.c // 128
    low = (tiles + 1) // 2 * 128

    def cols(k, way):
        cut = low if k % 2 == 0 else c.c - low
        return slice(0, cut) if way == 0 else slice(cut, c.c)

    sign = (1, -1)

    ag_sent = {0: [], 1: [], 2: []}

    def wblock(k, p, h, way):
        start = ring_row(mod8(p)) * nb + bands[h][0]
        return z.wb.at[k, rows16(start, bands[h][1]), cols(k, way)]

    def ag_wait(k, hop):
        for h in range(2):
            for way in range(2):
                dst = wblock(k, pos - sign[way] * (1 + hop), h, way)
                rcopy(dst, dst, z.ag_s.at[k, way, h, hop], z.ag_r.at[k, way, h, hop], ahead[way]).wait_recv()

    def ag(k, hop):
        for h in range(2):
            for way in range(2):
                origin = pos - sign[way] * hop
                dst = wblock(k, origin, h, way)
                if hop == 0:
                    src = w_ref.at[k, pl.ds(bands[h][0], bands[h][1]), cols(k, way)]
                else:
                    src = dst
                    rcopy(
                        dst, dst, z.ag_s.at[k, way, h, hop - 1], z.ag_r.at[k, way, h, hop - 1], ahead[way]
                    ).wait_recv()
                ag_sent[k].append(
                    send(src, dst, z.ag_s.at[k, way, h, hop], z.ag_r.at[k, way, h, hop], ahead[way])
                )

    grads = {}

    def rs(k, hop):
        for h in range(2):
            for way in range(2):
                owner = pos - sign[way] * (1 + hop)
                start = ring_row(mod8(owner)) * nb + bands[h][0]
                mine = grads[k].at[rows16(start, bands[h][1]), cols(k, way)]
                here = lambda i: z.slot.at[k, i, pl.ds(bands[h][0], bands[h][1]), cols(k, way)]
                src = mine
                if hop > 0:
                    src = here(hop - 1)
                    rcopy(
                        src, src, z.rs_s.at[k, way, h, hop - 1], z.rs_r.at[k, way, h, hop - 1], ahead[way]
                    ).wait_recv()
                    src[...] = (src[...].astype(F32) + mine[...].astype(F32)).astype(BF16)
                send(src, here(hop), z.rs_s.at[k, way, h, hop], z.rs_r.at[k, way, h, hop], ahead[way])

    def rs_end(k):
        for h in range(2):
            for way in range(2):
                src = z.slot.at[k, HOPS - 1, pl.ds(bands[h][0], bands[h][1]), cols(k, way)]
                rcopy(
                    src, src, z.rs_s.at[k, way, h, HOPS - 1], z.rs_r.at[k, way, h, HOPS - 1], ahead[way]
                ).wait_recv()
                mine = grads[k].at[rows16(row * nb + bands[h][0], bands[h][1]), cols(k, way)]
                z.fin[k, r, pl.ds(bands[h][0], bands[h][1]), cols(k, way)] = (
                    src[...].astype(F32) + mine[...].astype(F32)
                ).astype(BF16)

    def small(n, buf, hop, own=None):
        for way in range(2):
            if hop < 4 - way:
                if hop > 0:
                    small_wait(n, buf, hop - 1, way)
                blk = buf.at[ring_row(mod8(pos - sign[way] * hop))]
                src = blk if own is None or hop > 0 else own
                send(src, blk, z.sm_s.at[n, way, hop], z.sm_r.at[n, way, hop], ahead[way])

    def small_wait(n, buf, hop, way):
        blk = buf.at[ring_row(mod8(pos - sign[way] * (hop + 1)))]
        rcopy(blk, blk, z.sm_s.at[n, way, hop], z.sm_r.at[n, way, hop], ahead[way]).wait_recv()

    def share(n, buf, own=None):
        dst = buf.at[r]
        own = dst if own is None else own
        return [
            send(own, dst, z.ex_s.at[n, 0], z.ex_r.at[n, 0], cross_dev),
            send(own, dst, z.ex_s.at[n, 1], z.ex_r.at[n, 1], core_dev),
        ]

    def share_wait(n, buf, i):
        blk = buf.at[(cross, core, diag)[i]]
        rcopy(blk, blk, z.ex_s.at[n, i], z.ex_r.at[n, i], (cross_dev, core_dev, core_dev)[i]).wait_recv()

    def share_relay(n, buf):
        share_wait(n, buf, 0)
        blk = buf.at[cross]
        return send(blk, blk, z.ex_s.at[n, 2], z.ex_r.at[n, 2], core_dev)

    def sum_core(n, terms, i):
        image = (diag, core)[i]
        return send(terms.at[image], z.cr.at[n % 2, i], z.sum_s.at[n, i], z.sum_r.at[n, i], core_dev)

    def sum_wait(n, i):
        dst = (z.cr.at[n % 2, 0], z.cr.at[n % 2, 1], z.xr.at[n % 2])[i]
        rcopy(dst, dst, z.sum_s.at[n, i], z.sum_r.at[n, i], (core_dev, core_dev, cross_dev)[i]).wait_recv()

    def sum_cross(n, terms):
        sum_wait(n, 0)
        z.xs[...] = (terms[cross].astype(F32) + z.cr[n % 2, 0].astype(F32)).astype(BF16)
        return send(z.xs, z.xr.at[n % 2], z.sum_s.at[n, 2], z.sum_r.at[n, 2], cross_dev)

    def sum_take(n, terms, sl):
        return (
            terms[r, sl, :].astype(F32) + z.cr[n % 2, 1, sl, :].astype(F32) + z.xr[n % 2, sl, :].astype(F32)
        )

    def tiles_of(total, step, fn):
        def body(j, carry):
            fn(pl.ds(pl.multiple_of(j * step, step), step))
            return carry

        lax.fori_loop(0, total // step, body, 0)

    z.vb[row] = v_ref[...]
    small(0, z.vb, 0, v_ref)
    ag(0, 0)
    z.xa[r] = x_ref[...]
    z.ea[r] = e_ref[...]
    share(0, z.xa, x_ref)
    share(1, z.ea, e_ref)
    for k in range(3):
        z.wb[k, rows16(row * nb, nb), :] = w_ref[k]
    small(0, z.vb, 1)
    ag(0, 1)
    small(0, z.vb, 2)
    ag(0, 2)
    small(0, z.vb, 3)
    small_wait(0, z.vb, 3, 0)
    small_wait(0, z.vb, 2, 1)
    vec = z.vb[...].reshape(d, 128).astype(F32)
    z.vt[...] = jnp.transpose(vec)[0:16, :]
    ag(0, 3)

    def first_norm(i):
        def fn(sl):
            n, _ = normed(z.xa[i, sl, :].astype(F32))
            z.a1[i, sl, :] = (n * z.vt[0:1, :] + z.vt[1:2, :]).astype(BF16)

        tiles_of(t, 64, fn)

    first_norm(r)
    share_wait(0, z.xa, 1)
    first_norm(core)
    ag(0, 4)
    sent_x = share_relay(0, z.xa)
    ag(1, 0)
    first_norm(cross)
    ag(0, 5)
    share_wait(0, z.xa, 2)
    first_norm(diag)
    ag(0, 6)
    share_relay(1, z.ea)
    share_wait(1, z.ea, 1)
    ag(1, 1)
    ag_wait(0, 6)

    def swap(n, src, dst):
        for i, (who, dev) in enumerate(((cross, cross_dev), (diag, diag_dev), (core, core_dev))):
            send(src(who), dst.at[r], z.aa_s.at[n, i], z.aa_r.at[n, i], dev)

    def swap_wait(n, dst):
        for i, (who, dev) in enumerate(((cross, cross_dev), (diag, diag_dev), (core, core_dev))):
            blk = dst.at[who]
            rcopy(blk, blk, z.aa_s.at[n, i], z.aa_r.at[n, i], dev).wait_recv()

    swap(0, lambda who: z.wb.at[0, rows16(who * q, q), 0 : c.qp], z.wo4)
    z.wo4[r] = z.wb[0, rows16(r * q, q), 0 : c.qp]

    def of_rep(line):
        out = z.vt[line : line + 1, 0:q]
        for i in range(1, 4):
            out = jnp.where(r == i, z.vt[line : line + 1, i * q : (i + 1) * q], out)
        return out

    zero = jnp.zeros((1, q), F32)
    bias = jnp.concatenate([zero, of_rep(2), zero, of_rep(3)], axis=1)

    def project(i):
        z.pq[i] = (dot(z.a1[i], z.wb[0]) + bias).astype(BF16)

    def head(i, part, h):
        start = (part + 1) * q + h * HEAD_DIM
        return z.pq[i, :, start : start + HEAD_DIM]

    def attend(i):
        for h in range(heads):
            s = dot(head(i, 0, h), head(i, 1, h), 1, 1) * SCALE
            top = jnp.max(s, axis=-1, keepdims=True)
            ex = jnp.exp(s - top)
            total = jnp.sum(ex, axis=-1, keepdims=True)
            w = (ex * (1.0 / total)).astype(BF16)
            z.oq[i, :, h * HEAD_DIM : (h + 1) * HEAD_DIM] = dot(w, head(i, 2, h)).astype(BF16)
            z.lse[i, :, h : h + 1] = top + jnp.log(total)

    far_first = (diag, cross, core, r)
    near_first = (r, core, cross, diag)

    def pick(order, n):
        out = order[0]
        for i in range(1, 4):
            out = out + (n == i).astype(jnp.int32) * (order[i] - order[0])
        return out

    def in_order(order, fn, lo=0, hi=4):
        def body(n, carry):
            fn(pick(order, n))
            return carry

        lax.fori_loop(lo, hi, body, 0)

    in_order(far_first, project, 0, 2)
    ag(1, 2)
    in_order(far_first, project, 2, 4)
    in_order(far_first, attend, 0, 1)
    ag(1, 3)
    in_order(far_first, attend, 1, 2)
    ag(1, 4)
    in_order(far_first, attend, 2, 3)
    ag(1, 5)
    ag(2, 0)
    in_order(far_first, attend, 3, 4)
    swap_wait(0, z.wo4)
    for i in range(4):
        z.wo[:, i * q : (i + 1) * q] = z.wo4[i, :, 0:q]

    def out_term(i):
        z.part[i] = dot(z.oq[i, :, 0:q], z.wo[...]).astype(BF16)

    in_order(far_first, out_term)
    sent0 = [sum_core(0, z.part, 0), sum_core(0, z.part, 1)]
    ag(1, 6)
    sentx = sum_cross(0, z.part)
    ag(2, 1)
    ag_wait(1, 6)
    ag(2, 2)
    sum_wait(0, 1)
    sum_wait(0, 2)

    def middle(sl):
        m = x_ref[sl, :].astype(F32) + sum_take(0, z.part, sl) + z.vt[4:5, :]
        z.mid[sl, :] = m
        n, _ = normed(m)
        z.a2[r, sl, :] = (n * z.vt[5:6, :] + z.vt[6:7, :]).astype(BF16)

    tiles_of(t, 64, middle)
    share(2, z.a2)

    def up(i):
        u = dot(z.a2[i], z.wb[1]) + ub_ref[...]
        u2 = u * u
        th = jnp.tanh(ROOT_TWO_PI * (u * (1.0 + GELU_COEF * u2)))
        hp = 0.5 * (1.0 + th)
        z.act[i] = (u * hp).astype(BF16)
        z.der[i] = (
            hp + 0.5 * u * (1.0 - th * th) * (ROOT_TWO_PI * (1.0 + 3.0 * GELU_COEF * u2))
        ).astype(BF16)

    ag(2, 3)
    in_order(near_first, up, 0, 1)
    share_wait(2, z.a2, 1)
    ag(2, 4)
    in_order(near_first, up, 1, 2)
    ag(2, 5)
    share_relay(2, z.a2)
    in_order(near_first, up, 2, 3)
    ag(2, 6)
    share_wait(2, z.a2, 2)
    in_order(near_first, up, 3, 4)
    share_wait(1, z.ea, 2)

    def grad_of(dst, left, right):
        def fn(sl):
            acc = dot(left[0, :, sl], right[0], 0, 0)
            for i in range(1, 4):
                acc += dot(left[i, :, sl], right[i], 0, 0)
            dst[sl, :] = acc.astype(BF16)

        return fn

    tiles_of(d, 384, grad_of(z.gd, z.ea, z.act))
    ag_wait(2, 6)
    grads[0] = z.gd
    rs(0, 0)
    for cp in (*sent0, sentx):
        settle(cp)
    z.vg[row] = jnp.zeros((8, d), F32)

    def down_back(i):
        du = dot(z.ea[i], z.wb[2]) * z.der[i].astype(F32)
        z.vg[row, 3:4, :] += jnp.sum(du, axis=0, keepdims=True)
        dub = du.astype(BF16)
        z.der[i] = dub
        z.part[i] = dot(dub, z.wb[1], 1, 1).astype(BF16)

    in_order(far_first, down_back, 0, 1)
    sent1 = [sum_core(1, z.part, 0)]
    in_order(far_first, down_back, 1, 2)
    sentx = sum_cross(1, z.part)
    rs(0, 1)
    in_order(far_first, down_back, 2, 3)
    sent1.append(sum_core(1, z.part, 1))
    in_order(far_first, down_back, 3, 4)
    rs(0, 2)

    def out_back(i):
        z.act[i] = dot(z.act[i], z.wb[2], 1, 1).astype(BF16)

    in_order(far_first, out_back, 0, 2)
    rs(0, 3)
    in_order(far_first, out_back, 2, 4)
    sent2 = [sum_core(2, z.act, 0), sum_core(2, z.act, 1)]
    for cp in ag_sent[2]:
        settle(cp)
    grads[1] = z.wb.at[2]
    up_grad = grad_of(grads[1], z.a2, z.der)
    up_grad(pl.ds(0, 384))
    rs(0, 4)
    up_grad(pl.ds(384, 384))
    sum_wait(1, 1)
    sum_wait(1, 2)

    def second_norm(sl):
        da2 = sum_take(1, z.part, sl)
        e = e_ref[sl, :].astype(F32)
        n, inv = normed(z.mid[sl, :])
        dm = e + norm_back(da2 * z.vt[5:6, :], n, inv)
        z.dm[sl, :] = dm
        z.dmb[r, sl, :] = dm.astype(BF16)
        for line, val in ((4, dm), (5, da2 * n), (6, da2), (7, e)):
            z.vg[row, line : line + 1, :] += jnp.sum(val, axis=0, keepdims=True)

    tiles_of(t, 64, second_norm)
    sent3d = share(3, z.dmb)
    settle(sent_x)
    settle(sentx)
    sentx = sum_cross(2, z.act)
    rs(0, 5)
    up_grad(pl.ds(768, 384))
    rs(1, 0)

    def attend_back(i):
        z.do[i, :, 0:q] = dot(z.dmb[i], z.wo[...], 1, 1).astype(BF16)
        for h in range(heads):
            qh, kh, vh = (head(i, n, h) for n in range(3))
            g = z.do[i, :, h * HEAD_DIM : (h + 1) * HEAD_DIM]
            s = dot(qh, kh, 1, 1) * SCALE
            pr = jnp.exp(s - z.lse[i, :, h : h + 1])
            dv = dot(pr.astype(BF16), g, 0, 0)
            dpr = dot(g, vh, 1, 1)
            delta = jnp.sum(pr * dpr, axis=-1, keepdims=True)
            ds = (pr * (dpr - delta) * SCALE).astype(BF16)
            for n, val in enumerate((dot(ds, kh), dot(ds, qh, 0, 0), dv)):
                start = (n + 1) * q + h * HEAD_DIM
                z.xa[i, :, start : start + HEAD_DIM] = val.astype(BF16)
        z.vg[row, 2:3, :] += jnp.sum(z.xa[i].astype(F32), axis=0, keepdims=True)

    in_order(near_first, attend_back, 0, 1)
    share_wait(3, z.dmb, 1)
    rs(0, 6)
    in_order(near_first, attend_back, 1, 2)
    rs(1, 1)
    share_relay(3, z.dmb)
    rs_end(0)
    share(4, z.fin.at[0])
    in_order(near_first, attend_back, 2, 3)
    rs(1, 2)
    share_wait(3, z.dmb, 2)
    in_order(near_first, attend_back, 3, 4)
    rs(1, 3)

    og = dot(z.oq[0, :, 0:q], z.dmb[0], 0, 0)
    for i in range(1, 4):
        og += dot(z.oq[i, :, 0:q], z.dmb[i], 0, 0)
    for i in range(4):
        z.ogs[i, :, 0:q] = og[:, i * q : (i + 1) * q].astype(BF16)
    swap(1, lambda who: z.ogs.at[who], z.wo4)
    z.wo4[r] = z.ogs[r]
    for cp in ag_sent[1]:
        settle(cp)
    for cp in sent1:
        settle(cp)
    rs(1, 4)

    def first_back(i):
        z.part[i, :, :] = dot(z.xa[i, :, q:], z.wb[0, :, q:], 1, 1).astype(BF16)

    in_order(far_first, first_back, 0, 2)
    sent3 = [sum_core(3, z.part, 0)]
    rs(1, 5)
    in_order(far_first, first_back, 2, 4)
    sent3.append(sum_core(3, z.part, 1))
    sum_wait(2, 1)
    sum_wait(2, 2)

    def last_out(sl):
        z.xs[sl, :] = (z.mid[sl, :] + sum_take(2, z.act, sl) + z.vt[7:8, :]).astype(BF16)

    settle(sentx)
    tiles_of(t, 64, last_out)
    copies = []

    def put(n, src, dst):
        cp = pltpu.make_async_copy(src, dst, z.out_s.at[n])
        cp.start()
        copies.append(cp)
        return cp

    put(0, z.xs, out_ref).wait()
    copies.pop()
    sentx = sum_cross(3, z.part)
    grads[2] = z.wb.at[1]
    tiles_of(d, 384, grad_of(grads[2], z.a1, z.xa))
    swap_wait(1, z.wo4)
    for i in range(4):
        grads[2][i * q : (i + 1) * q, 0:q] = z.wo4[i, :, 0:q]
    rs(1, 6)
    rs(2, 0)
    share_relay(4, z.fin.at[0])
    rs_end(1)
    share(5, z.fin.at[1])
    rs(2, 1)
    sum_wait(3, 1)
    sum_wait(3, 2)

    def last_norm(sl):
        da1 = sum_take(3, z.part, sl)
        n, inv = normed(x_ref[sl, :].astype(F32))
        z.dmb[r, sl, :] = (z.dm[sl, :] + norm_back(da1 * z.vt[0:1, :], n, inv)).astype(BF16)
        for line, val in ((0, da1 * n), (1, da1)):
            z.vg[row, line : line + 1, :] += jnp.sum(val, axis=0, keepdims=True)

    for cp in sent3d:
        settle(cp)
    tiles_of(t, 64, last_norm)
    put(1, z.dmb.at[r], ing_ref)
    small(1, z.vg, 0)
    rs(2, 2)
    small(1, z.vg, 1)
    rs(2, 3)
    small(1, z.vg, 2)
    share_relay(5, z.fin.at[1])
    rs(2, 4)
    small(1, z.vg, 3)
    rs(2, 5)
    small_wait(1, z.vg, 3, 0)
    small_wait(1, z.vg, 2, 1)
    total = z.vg[0]
    for i in range(1, RING):
        total += z.vg[i]
    z.vf[r] = total
    share(7, z.vf)
    rs(2, 6)
    for k in range(2):
        share_wait(4 + k, z.fin.at[k], 1)
        share_wait(4 + k, z.fin.at[k], 2)
        put(2 + k, z.fin.at[k], (g0_ref, g1_ref)[k])
    share_relay(7, z.vf)
    share_wait(7, z.vf, 1)
    share_wait(7, z.vf, 2)
    put(5, z.vf, vo_ref)
    rs_end(2)
    share(6, z.fin.at[2])
    share_relay(6, z.fin.at[2])
    share_wait(6, z.fin.at[2], 1)
    share_wait(6, z.fin.at[2], 2)
    put(4, z.fin.at[2], g2_ref)
    for cp in list(pending.values()):
        settle(cp)
    for cp in copies:
        cp.wait()


def per_device(reps, shards, images, cotangent, w_qkv, w_out, w_up, w_down, vectors, up_bias):
    r = lax.axis_index("rep")
    batch, seq, d = images.shape
    q = d // reps
    hidden = w_up.shape[1]
    ffq = hidden // reps
    wide = -(-max(4 * q, ffq) // 128) * 128
    sub = shards // RING
    groups = [[i * sub + j for j in range(sub)] for i in range(RING)]
    shard = lax.axis_index("shard")

    def take(w, start, size):
        return lax.dynamic_slice_in_dim(w, start, size, 1)

    first = [take(w_out, r * q, q)] + [take(w_qkv, k * d + r * q, q) for k in range(3)]
    pad = ((0, 0), (0, wide - ffq))
    w = jnp.stack(
        [
            jnp.concatenate(first, axis=1),
            jnp.pad(take(w_up, r * ffq, ffq), pad),
            jnp.pad(take(w_down, r * ffq, ffq), pad),
        ]
    )
    v = jnp.pad(vectors, ((0, 0), (0, 128 - vectors.shape[1])))
    if sub > 1:
        w = lax.all_gather(w, "shard", axis=1, tiled=True, axis_index_groups=groups)
        v = lax.all_gather(v, "shard", axis=0, tiled=True, axis_index_groups=groups)
    ub = lax.dynamic_slice_in_dim(up_bias, r * ffq, ffq, 0).astype(F32)
    ub = jnp.pad(ub, (0, wide - ffq)).reshape(1, wide)
    c = Sizes(d, seq, wide, w.shape[1], sub)
    vmem = pl.BlockSpec(memory_space=pltpu.VMEM)
    hbm = pl.BlockSpec(memory_space=pl.ANY)
    grad = jax.ShapeDtypeStruct((4, c.b, wide), BF16)
    tok = jax.ShapeDtypeStruct((seq, d), BF16)
    outputs, input_grad, g_down, g_up, g_first, vf = pl.pallas_call(
        functools.partial(kernel, c),
        out_shape=(tok, tok, grad, grad, grad, jax.ShapeDtypeStruct((4, 8, d), F32)),
        in_specs=[vmem] * 5,
        out_specs=(hbm,) * 6,
        scratch_shapes=[make(c) for make in SCRATCH.values()],
        compiler_params=pltpu.CompilerParams(
            collective_id=0, has_side_effects=True, vmem_limit_bytes=67043328
        ),
    )(w, images.reshape(seq, d), cotangent.reshape(seq, d), v, ub)

    def finish(g):
        g = g.astype(F32)
        if sub > 1:
            g = lax.psum_scatter(g, "shard", scatter_dimension=1, tiled=True, axis_index_groups=groups)
        return g

    def columns(g):
        return jnp.concatenate([g[i, :, :ffq] for i in range(reps)], axis=1)

    g_down, g_up, g_first = finish(g_down), finish(g_up), finish(g_first)
    g_out = jnp.concatenate([g_first[i, :, :q] for i in range(reps)], axis=1)
    g_qkv = jnp.concatenate(
        [g_first[i, :, k * q : (k + 1) * q] for k in range(1, 4) for i in range(reps)], axis=1
    )
    if sub > 1:
        vf = lax.psum(vf, "shard", axis_index_groups=groups)
    whole = jnp.sum(vf, axis=0)
    bias = [jnp.concatenate([vf[i, 2, k * q : (k + 1) * q] for i in range(reps)]) for k in (1, 3)]
    upb = jnp.concatenate([vf[i, 3, :ffq] for i in range(reps)])
    lines = jnp.stack([whole[0], whole[1], *bias, whole[4], whole[5], whole[6], whole[7]], axis=1)
    own = d // shards
    vec = lax.dynamic_slice_in_dim(lines, shard * own, own, 0)
    shape = (batch, seq, d)
    return (
        outputs.reshape(shape),
        input_grad.reshape(shape),
        g_qkv,
        g_out,
        columns(g_up),
        columns(g_down),
        vec,
        upb,
    )


def solution(mesh):
    reps, shards = mesh.shape["rep"], mesh.shape["shard"]
    token = P(("rep", "shard"), None, None)
    line = P("shard", None)

    def body(*args):
        return per_device(reps, shards, *args)

    return jax.shard_map(
        body,
        mesh=mesh,
        in_specs=(token, token, line, line, line, line, line, P()),
        out_specs=(token, token, line, line, line, line, line, P()),
        check_vma=False,
    )
```

time: 939 us -> 269 us (0.29)
  waiting for transfers between devices: 645 us -> 0 us
  Pallas kernels: 0 us -> 236 us
  matrix products: 96.5 us -> 0 us
  blocking collectives: 75.6 us -> 0 us
  local copies, waits for them, and re-layouts: 63.5 us -> 23.2 us
  other arithmetic: 30.9 us -> 5.21 us
  between operations: 15.9 us -> 0.94 us
    reduce_scatter x8 -> x0, waiting for transfers between devices: 303 us -> none  [the longest x3 158 us: reduce_rows(): lax.psum_scatter(term.astype(BF16), 'shard', scatter_dimension=0, tiled=T...]
    all_gather x10 -> x0, waiting for transfers between devices: 256 us -> none  [the longest x4 92.5 us: gather_rep(): return lax.all_gather(a, 'rep', axis=0, tiled=True)]
    pallas_call x0 -> x1, Pallas kernels: none -> 236 us  [per_device(): pl.pallas_call(functools.partial(kernel, c), out_shape=(tok, tok, grad, g...]
    dot_general x18 -> x0, matrix products: 96.5 us -> none  [the longest x12 71 us: dot(): lax.dot_general(a, b, (((ca,), (cb,)), ((), ())), preferred_element_type=...]
    unnamed x21 -> x0, waiting for transfers between devices: 64.9 us -> none
    all_gather x2 -> x0, blocking collectives: 43 us -> none  [the longest x1 32.7 us: per_device(): params = lax.all_gather(vectors, 'shard', axis=0, tiled=True).astype(F32)]
    psum x2 -> x0, blocking collectives: 32.6 us -> none  [the longest x1 21.7 us: per_device(): upb = lax.all_gather(lax.psum(upb, 'shard'), 'rep', axis=0, tiled=True)]
    reshape x11 -> x1, local copies, waits for them, and re-layouts: 32.9 us -> 0.6 us  [per_device(): ub = jnp.pad(ub, (0, wide - ffq)).reshape(1, wide)]
  transfers between devices with their start and end apart: 20 -> 0, of which waited for: 18 -> 0; matrix products, arithmetic and copies ran while one was open for 17% -> 0% of each run, Pallas kernels for 0% -> 0%
where the time goes in v2:
time: 269 us; the launch traced here: 265 us
  Pallas kernels  236 us (88%)
  local copies, waits for them, and re-layouts  23.2 us (9%)
  other arithmetic  5.21 us (2%)
    pallas_call x1, Pallas kernels, per_device(): pl.pallas_call(functools.partial(kernel, c), out_shape=(tok, tok, grad, g...  236 us

profile of v2, /device:TPU:0, one launch (start us, length us, event | category | flops | bytes accessed | tf_op | source)
XLA Modules:
  0.0 265.2 jit_solution(6298667601733809152)
XLA Ops:
  0.6 0.8 dynamic_slice.30
  1.4 0.6 reshape.40.ub_ref
  2.0 0.8 copy.16
  2.8 0.6 pad.18.v_ref
  3.5 1.3 constant_dynamic-slice_fusion.3
  4.8 0.2 concatenate.24
  5.1 1.4 constant_dynamic-slice_fusion.1
  6.5 1.1 pad_maximum_fusion.w_ref
  7.6 235.9 %shard_map.143 = (bf16[256,1152]{1,0:T(8,128)(2,1)}, bf16[256,1152]{1,0:T(8,128)(2,1)}, bf16[4,144,1152]{2,1,0:T(8,128)(2,1)}, bf16[4,144,1152]{2,1,0:T(8,128)(2...) custom-call(bf16[3,144,1152]{2,1,0:T(8,128)(2,1)} %pad_maximum_fusion.w_ref, bf16[256,1152]{1,0:T(8,128)(2,1)} %bitcast.70, ...), custom_call_target="tpu_custom_call" | custom-call | tf_op jit(solution)/shard_map/pallas_call | solution.py:663
  243.5 0.9 slice_reduce_fusion.4
  244.4 0.1 concatenate.30
  244.5 0.1 concatenate.29
  244.6 0.9 slice_reduce_fusion
  245.5 0.9 reduce_sum.9
  246.4 0.1 stack.27
  246.5 0.7 constant_dynamic-slice_fusion
  247.2 0.7 concatenate.31
  247.9 1.5 convert_element_type.17
  249.4 1.5 slice_bitcast_fusion.8
  250.9 1.1 concatenate.26
  252.0 0.0 copy-start
  252.0 3.4 %concatenate.25 = f32[144,3456]{1,0:T(8,128)} concatenate(f32[144,288]{1,0:T(8,128)} %get-tuple-element.55, f32[144,288]{1,0:T(8,128)} %get-tuple-element.54, f32[144,288]{1,0:T(8,128)S(1)} %get-tuple-element.53, f32[144,288]{1,0:T(8,128)S(1)} %get-tuple-element.52, f32[144,288]{1,0:T(8,128)S(1)} %get-tuple-element.51, f32[144,288]{1,0:T(8,128)S(1)} %get-tuple-element.50, ...), dimensions={1} | concatenate | bytes 3981312 | tf_op jit(solution)/shard_map/concatenate | solution.py:685
  255.4 0.0 copy-done
  255.4 0.2 convert_element_type.18
  255.6 0.2 slice_bitcast_fusion.4
  255.7 2.4 concatenate.27
  258.2 1.5 convert_element_type.19
  259.7 0.2 slice_bitcast_fusion
  259.9 0.0 copy-start.1
  259.9 2.4 concatenate.28
  262.3 1.9 copy.19
  264.2 0.0 copy-done.1
  264.2 0.8 copy.20
  (6 shorter events, 0.1 us)
Async XLA Ops:
  252.0 3.4 %copy-start = (bf16[4,144,1152]{2,1,0:T(8,128)(2,1)S(1)}, bf16[4,144,1152]{2,1,0:T(8,128)(2,1)}, u32[]{:S(2)}) copy-start(bf16[4,144,1152]{2,1,0:T(8,128)(2,1)} %get-tuple-element.17) | copy-start | bytes 3981316
  259.9 4.4 %copy-start.1 = (bf16[256,1152]{1,0:T(8,128)(2,1)S(1)}, bf16[256,1152]{1,0:T(8,128)(2,1)}, u32[]{:S(2)}) copy-start(bf16[256,1152]{1,0:T(8,128)(2,1)} %get-tuple-element.15) | copy-start | bytes 1769476

commit v3 on v2

v3 whole, which is shorter than its diff:
```python
import functools
import math

import jax
import jax.numpy as jnp
from jax import lax
from jax.experimental import pallas as pl
from jax.experimental.pallas import tpu as pltpu
from jax.sharding import PartitionSpec as P

HEAD_DIM = 72
EPSILON = 1e-06
GELU_COEF = 0.044715
ROOT_TWO_PI = math.sqrt(2.0 / math.pi)
SCALE = 1.0 / math.sqrt(HEAD_DIM)
F32 = jnp.float32
BF16 = jnp.bfloat16
RING = 8
HOPS = RING - 1
BANDS = 3


def dot(a, b, ca=1, cb=0):
    return lax.dot_general(a, b, (((ca,), (cb,)), ((), ())), preferred_element_type=F32)


def ring_row(pos):
    return 2 * pos + (pos // 4) * (15 - 4 * pos)


def mod8(v):
    return lax.rem(v + 4 * RING, RING)


def rows16(start, size):
    return pl.ds(pl.multiple_of(start, 16), size)


def normed(x):
    mean = jnp.mean(x, axis=-1, keepdims=True)
    cen = x - mean
    inv = lax.rsqrt(jnp.mean(cen * cen, axis=-1, keepdims=True) + EPSILON)
    return cen * inv, inv


def norm_back(dn, n, inv):
    a = jnp.mean(dn, axis=-1, keepdims=True)
    b = jnp.mean(dn * n, axis=-1, keepdims=True)
    return inv * (dn - a - n * b)


SCRATCH = dict(
    raw=lambda c: pltpu.VMEM((2, c.b, c.hidden), BF16),
    wb=lambda c: pltpu.VMEM((3, c.d, c.c), BF16),
    wo4=lambda c: pltpu.VMEM((4, c.q, c.qp), BF16),
    wo=lambda c: pltpu.VMEM((c.q, c.d), BF16),
    xa=lambda c: pltpu.VMEM((4, c.t, c.c), BF16),
    ea=lambda c: pltpu.VMEM((4, c.t, c.d), BF16),
    a1=lambda c: pltpu.VMEM((4, c.t, c.d), BF16),
    a2=lambda c: pltpu.VMEM((4, c.t, c.d), BF16),
    dmb=lambda c: pltpu.VMEM((4, c.t, c.d), BF16),
    pq=lambda c: pltpu.VMEM((4, c.t, c.c), BF16),
    oq=lambda c: pltpu.VMEM((4, c.t, c.qp), BF16),
    lse=lambda c: pltpu.VMEM((4, c.t, 128), F32),
    act=lambda c: pltpu.VMEM((4, c.t, c.c), BF16),
    der=lambda c: pltpu.VMEM((4, c.t, c.c), BF16),
    mid=lambda c: pltpu.VMEM((c.t, c.d), F32),
    dm=lambda c: pltpu.VMEM((c.t, c.d), F32),
    do=lambda c: pltpu.VMEM((c.t, c.qp), BF16),
    part=lambda c: pltpu.VMEM((4, c.t, c.d), BF16),
    xs=lambda c: pltpu.VMEM((2, c.t, c.d), BF16),
    cr=lambda c: pltpu.VMEM((2, 2, c.t, c.d), BF16),
    xr=lambda c: pltpu.VMEM((2, c.t, c.d), BF16),
    gd=lambda c: pltpu.VMEM((c.d, c.c), BF16),
    slot=lambda c: pltpu.VMEM((3, HOPS, c.b, c.c), BF16),
    fin=lambda c: pltpu.VMEM((3, 4, c.b, c.c), BF16),
    ogs=lambda c: pltpu.VMEM((4, c.q, c.qp), BF16),
    vb=lambda c: pltpu.VMEM((RING, 8, c.b), F32),
    vt=lambda c: pltpu.VMEM((8, c.d), F32),
    ub=lambda c: pltpu.VMEM((8, c.c), F32),
    vg=lambda c: pltpu.VMEM((RING, 8, c.d), F32),
    vf=lambda c: pltpu.VMEM((4, 8, c.d), F32),
    ag_s=lambda c: pltpu.SemaphoreType.DMA((3, 2, BANDS, HOPS)),
    ag_r=lambda c: pltpu.SemaphoreType.DMA((3, 2, BANDS, HOPS)),
    rs_s=lambda c: pltpu.SemaphoreType.DMA((3, 2, BANDS, HOPS)),
    rs_r=lambda c: pltpu.SemaphoreType.DMA((3, 2, BANDS, HOPS)),
    sm_s=lambda c: pltpu.SemaphoreType.DMA((2, 2, 4)),
    sm_r=lambda c: pltpu.SemaphoreType.DMA((2, 2, 4)),
    ex_s=lambda c: pltpu.SemaphoreType.DMA((10, 3)),
    ex_r=lambda c: pltpu.SemaphoreType.DMA((10, 3)),
    sum_s=lambda c: pltpu.SemaphoreType.DMA((4, 3)),
    sum_r=lambda c: pltpu.SemaphoreType.DMA((4, 3)),
    aa_s=lambda c: pltpu.SemaphoreType.DMA((2, 3)),
    aa_r=lambda c: pltpu.SemaphoreType.DMA((2, 3)),
    in_s=lambda c: pltpu.SemaphoreType.DMA((6,)),
    out_s=lambda c: pltpu.SemaphoreType.DMA((6,)),
)


class Sizes:
    def __init__(self, d, t, c, b, sub, hidden):
        self.d, self.t, self.c, self.b, self.sub, self.hidden = d, t, c, b, sub, hidden
        self.q = d // 4
        self.f = hidden // 4
        self.qp = -(-self.q // 128) * 128
        self.heads = self.q // HEAD_DIM


def kernel(
    c, wq_ref, wo_ref, wu_ref, wd_ref, x_ref, e_ref, v_ref, ub_ref,
    out_ref, ing_ref, g0_ref, g1_ref, g2_ref, vo_ref, *refs
):
    z = type("Refs", (), dict(zip(SCRATCH, refs)))
    d, t, nb, q, heads = c.d, c.t, c.b, c.q, c.heads
    band = nb // BANDS
    r = lax.axis_index("rep")
    shard = lax.axis_index("shard")
    row, sub = shard // c.sub, lax.rem(shard, c.sub)
    za, yb = row // 2, lax.rem(row, 2)
    pos = za + yb * (7 - 2 * za)

    def ring_dev(p):
        return (r, ring_row(mod8(p)) * c.sub + sub)

    ahead = (ring_dev(pos + 1), ring_dev(pos - 1))
    core = r + 1 - 2 * lax.rem(r, 2)
    cross = lax.rem(r + 2, 4)
    diag = lax.rem(core + 2, 4)
    core_dev, cross_dev, diag_dev = (core, shard), (cross, shard), (diag, shard)
    sign = (1, -1)

    def rcopy(src, dst, kind, index, dev):
        return pltpu.make_async_remote_copy(
            src_ref=src, dst_ref=dst,
            send_sem=getattr(z, kind + "_s").at[index], recv_sem=getattr(z, kind + "_r").at[index],
            device_id=dev, device_id_type=pl.DeviceIdType.MESH,
        )

    def send(src, dst, kind, index, dev):
        rcopy(src, dst, kind, index, dev).start()

    def recv(dst, kind, index, dev):
        rcopy(dst, dst, kind, index, dev).wait_recv()

    def sent(src, kind, index, dev):
        rcopy(src, src, kind, index, dev).wait_send()

    def repeat(count, fn, lo=0):
        def body(n, carry):
            fn(n)
            return carry

        lax.fori_loop(lo, count, body, 0)

    def tiles_of(total, step, fn):
        repeat(total // step, lambda j: fn(pl.ds(pl.multiple_of(j * step, step), step)))

    low = (c.c // 128 + 1) // 2 * 128

    def cols(k, way):
        cut = low if k % 2 == 0 else c.c - low
        return slice(0, cut) if way == 0 else slice(cut, c.c)

    def wblock(k, p, h, way):
        return z.wb.at[k, rows16(ring_row(mod8(p)) * nb + h * band, band), cols(k, way)]

    def ag(k, hop):
        def one(h):
            for way in range(2):
                blk = wblock(k, pos - sign[way] * hop, h, way)
                if not (isinstance(hop, int) and hop == 0):
                    recv(blk, "ag", (k, way, h, hop - 1), ahead[way])
                send(blk, blk, "ag", (k, way, h, hop), ahead[way])

        repeat(BANDS, one)

    def ag_wait(k):
        def one(h):
            for way in range(2):
                recv(wblock(k, pos - sign[way] * RING, h, way), "ag", (k, way, h, HOPS - 1), ahead[way])

        repeat(BANDS, one)

    def ag_sent(k):
        def one(n):
            for way in range(2):
                sent(wblock(k, pos, n // HOPS, way), "ag", (k, way, n // HOPS, lax.rem(n, HOPS)), ahead[way])

        repeat(BANDS * HOPS, one)

    grads = {0: z.gd, 1: z.wb.at[2], 2: z.wb.at[1]}

    def slot(k, hop, h, way):
        return z.slot.at[k, hop, rows16(h * band, band), cols(k, way)]

    def term(k, p, h, way):
        return grads[k].at[rows16(ring_row(mod8(p)) * nb + h * band, band), cols(k, way)]

    def rs(k, hop):
        def one(h):
            for way in range(2):
                src = mine = term(k, pos - sign[way] * (1 + hop), h, way)
                if not (isinstance(hop, int) and hop == 0):
                    src = slot(k, hop - 1, h, way)
                    recv(src, "rs", (k, way, h, hop - 1), ahead[way])
                    src[...] = (src[...].astype(F32) + mine[...].astype(F32)).astype(BF16)
                send(src, slot(k, hop, h, way), "rs", (k, way, h, hop), ahead[way])

        repeat(BANDS, one)

    def rs_end(k, h):
        for way in range(2):
            src = slot(k, HOPS - 1, h, way)
            recv(src, "rs", (k, way, h, HOPS - 1), ahead[way])
            z.fin[k, r, rows16(h * band, band), cols(k, way)] = (
                src[...].astype(F32) + term(k, pos, h, way)[...].astype(F32)
            ).astype(BF16)

    def rs_sent(k):
        def one(n):
            for way in range(2):
                sent(slot(k, 0, n // HOPS, way), "rs", (k, way, n // HOPS, lax.rem(n, HOPS)), ahead[way])

        repeat(BANDS * HOPS, one)

    def small(n, buf, hop):
        for way in range(2):
            if hop < 4 - way:
                if hop > 0:
                    small_wait(n, buf, hop - 1, way)
                blk = buf.at[ring_row(mod8(pos - sign[way] * hop))]
                send(blk, blk, "sm", (n, way, hop), ahead[way])

    def small_wait(n, buf, hop, way):
        recv(buf.at[ring_row(mod8(pos - sign[way] * (hop + 1)))], "sm", (n, way, hop), ahead[way])

    def small_sent(n, buf):
        for way in range(2):
            for hop in range(4 - way):
                sent(buf.at[row], "sm", (n, way, hop), ahead[way])

    ex_dev = (cross_dev, core_dev, core_dev)

    def share(n, at, own=None):
        for i in range(2):
            send(at(r) if own is None else own, at(r), "ex", (n, i), ex_dev[i])

    def share_wait(n, at, i):
        recv(at((cross, core, diag)[i]), "ex", (n, i), ex_dev[i])

    def share_relay(n, at):
        share_wait(n, at, 0)
        send(at(cross), at(cross), "ex", (n, 2), core_dev)

    def share_sent(n, at):
        for i in range(3):
            sent(at(r), "ex", (n, i), ex_dev[i])

    def image_of(buf):
        return lambda i: buf.at[i]

    sum_dev = (core_dev, core_dev, cross_dev)

    def sum_core(n, terms, i):
        send(terms.at[(diag, core)[i]], z.cr.at[n % 2, i], "sum", (n, i), core_dev)

    def sum_wait(n, i):
        recv((z.cr.at[n % 2, 0], z.cr.at[n % 2, 1], z.xr.at[n % 2])[i], "sum", (n, i), sum_dev[i])

    def sum_cross(n, terms):
        sum_wait(n, 0)

        def add(sl):
            z.xs[n % 2, sl, :] = (
                terms[cross, sl, :].astype(F32) + z.cr[n % 2, 0, sl, :].astype(F32)
            ).astype(BF16)

        tiles_of(t, 64, add)
        send(z.xs.at[n % 2], z.xr.at[n % 2], "sum", (n, 2), cross_dev)

    def sum_take(n, terms, sl):
        return (
            terms[r, sl, :].astype(F32) + z.cr[n % 2, 1, sl, :].astype(F32) + z.xr[n % 2, sl, :].astype(F32)
        )

    def sum_sent(n):
        for i in range(3):
            sent(z.xr.at[0], "sum", (n, i), sum_dev[i])

    aa = ((cross, cross_dev), (diag, diag_dev), (core, core_dev))

    def swap(n, src):
        for i, (who, dev) in enumerate(aa):
            send(src(who), z.wo4.at[r], "aa", (n, i), dev)

    def swap_wait(n):
        for i, (who, dev) in enumerate(aa):
            recv(z.wo4.at[who], "aa", (n, i), dev)

    def swap_sent(n):
        for i, (who, dev) in enumerate(aa):
            sent(z.wo4.at[r], "aa", (n, i), dev)

    far_first = (diag, cross, core, r)
    near_first = (r, core, cross, diag)

    def pick(order, n):
        out = order[0]
        for i in range(1, 4):
            out = out + (n == i).astype(jnp.int32) * (order[i] - order[0])
        return out

    loads = [pltpu.make_async_copy(wo_ref, z.slot.at[0, 3], z.in_s.at[3])]
    for k in range(3):
        loads.append(pltpu.make_async_copy(wq_ref.at[:, k * d : (k + 1) * d], z.slot.at[0, k], z.in_s.at[k]))
    for k, ref in enumerate((wu_ref, wd_ref)):
        loads.append(pltpu.make_async_copy(ref, z.raw.at[k], z.in_s.at[4 + k]))
    for cp in loads:
        cp.start()
    z.vb[row] = v_ref[...].astype(F32)
    z.xa[r] = x_ref[...]
    z.ea[r] = e_ref[...]
    barrier = pltpu.get_barrier_semaphore()
    peers = (*ahead, core_dev, cross_dev, diag_dev)
    for dev in peers:
        pl.semaphore_signal(barrier, inc=1, device_id=dev, device_id_type=pl.DeviceIdType.MESH)
    pl.semaphore_wait(barrier, len(peers))
    xa, ea, a2s, dms = (image_of(b) for b in (z.xa, z.ea, z.a2, z.dmb))
    share(0, xa, x_ref)
    small(0, z.vb, 0)
    share(1, ea, e_ref)
    own = rows16(row * nb, nb)
    for cp in loads[:4]:
        cp.wait()
    for i in range(4):

        @pl.when(r == i)
        def _():
            for k in range(4):
                z.wb[0, own, k * q : (k + 1) * q] = z.slot[0, (k + 3) % 4, :, i * q : (i + 1) * q]

    ag(0, 0)
    for cp in loads[4:]:
        cp.wait()
    z.ub[...] = jnp.zeros_like(z.ub)
    for i in range(4):

        @pl.when(r == i)
        def _():
            for k in range(2):
                z.wb[1 + k, own, 0 : c.f] = z.raw[k, :, i * c.f : (i + 1) * c.f]
            z.ub[0:1, 0 : c.f] = ub_ref[0:1, i * c.f : (i + 1) * c.f].astype(F32)

    for k in range(2):
        z.wb[1 + k, own, c.f :] = jnp.zeros((nb, c.c - c.f), BF16)

    small(0, z.vb, 1)
    ag(0, 1)
    small(0, z.vb, 2)
    ag(0, 2)
    small(0, z.vb, 3)
    small_wait(0, z.vb, 3, 0)
    small_wait(0, z.vb, 2, 1)
    for s in range(RING):
        z.vt[:, s * nb : (s + 1) * nb] = z.vb[s]
    ag(0, 3)

    def first_norm(i):
        def fn(sl):
            n, _ = normed(z.xa[i, sl, :].astype(F32))
            z.a1[i, sl, :] = (n * z.vt[0:1, :] + z.vt[1:2, :]).astype(BF16)

        tiles_of(t, 64, fn)

    first_norm(r)
    share_wait(0, xa, 1)
    first_norm(core)
    ag(0, 4)
    share_relay(0, xa)
    first_norm(cross)
    ag(0, 5)
    share_wait(0, xa, 2)
    ag(1, 0)
    first_norm(diag)
    ag(0, 6)
    ag(2, 0)
    ag_wait(0)
    swap(0, lambda who: z.wb.at[0, rows16(who * q, q), 0 : c.qp])
    z.wo4[r] = z.wb[0, rows16(r * q, q), 0 : c.qp]

    def of_rep(line):
        out = z.vt[line : line + 1, 0:q]
        for i in range(1, 4):
            out = jnp.where(r == i, z.vt[line : line + 1, i * q : (i + 1) * q], out)
        return out

    z.ub[1:2, :] = jnp.zeros((1, c.c), F32)
    z.ub[1:2, q : 2 * q] = of_rep(2)
    z.ub[1:2, 3 * q : 4 * q] = of_rep(3)

    def head(i, part, h):
        start = (part + 1) * q + h * HEAD_DIM
        return z.pq[i, :, start : start + HEAD_DIM]

    def attention(n):
        i = pick(far_first, n)
        z.pq[i] = (dot(z.a1[i], z.wb[0]) + z.ub[1:2, :]).astype(BF16)
        ag(1, n + 1)
        for h in range(heads):
            s = dot(head(i, 0, h), head(i, 1, h), 1, 1) * SCALE
            top = jnp.max(s, axis=-1, keepdims=True)
            ex = jnp.exp(s - top)
            total = jnp.sum(ex, axis=-1, keepdims=True)
            w = (ex * (1.0 / total)).astype(BF16)
            z.oq[i, :, h * HEAD_DIM : (h + 1) * HEAD_DIM] = dot(w, head(i, 2, h)).astype(BF16)
            z.lse[i, :, h : h + 1] = top + jnp.log(total)

    repeat(4, attention)
    share_relay(1, ea)
    swap_wait(0)
    for i in range(4):
        z.wo[:, i * q : (i + 1) * q] = z.wo4[i, :, 0:q]

    def out_term(n):
        i = pick(far_first, n)
        z.part[i] = dot(z.oq[i, :, 0:q], z.wo[...]).astype(BF16)
        pl.when(n == 0)(lambda: sum_core(0, z.part, 0))
        pl.when(n == 1)(lambda: sum_cross(0, z.part))
        pl.when(n == 2)(lambda: sum_core(0, z.part, 1))

    repeat(4, out_term)
    ag(1, 5)
    ag(2, 1)
    ag(1, 6)
    ag(2, 2)
    sum_wait(0, 1)
    sum_wait(0, 2)

    def middle(sl):
        m = x_ref[sl, :].astype(F32) + sum_take(0, z.part, sl) + z.vt[4:5, :]
        z.mid[sl, :] = m
        n, _ = normed(m)
        z.a2[r, sl, :] = (n * z.vt[5:6, :] + z.vt[6:7, :]).astype(BF16)

    tiles_of(t, 64, middle)
    share(2, a2s)
    ag_wait(1)

    def up(n):
        i = pick(near_first, n)
        ag(2, n + 3)
        pl.when(n == 1)(lambda: share_wait(2, a2s, 1))
        pl.when(n == 2)(lambda: share_relay(2, a2s))
        pl.when(n == 3)(lambda: share_wait(2, a2s, 2))
        u = dot(z.a2[i], z.wb[1]) + z.ub[0:1, :]
        u2 = u * u
        th = jnp.tanh(ROOT_TWO_PI * (u * (1.0 + GELU_COEF * u2)))
        hp = 0.5 * (1.0 + th)
        z.act[i] = (u * hp).astype(BF16)
        z.der[i] = (
            hp + 0.5 * u * (1.0 - th * th) * (ROOT_TWO_PI * (1.0 + 3.0 * GELU_COEF * u2))
        ).astype(BF16)

    repeat(4, up)
    share_wait(1, ea, 1)
    share_wait(1, ea, 2)

    def grad_of(dst, left, right):
        def fn(sl):
            acc = dot(left[0, :, sl], right[0], 0, 0)
            for i in range(1, 4):
                acc += dot(left[i, :, sl], right[i], 0, 0)
            dst[sl, :] = acc.astype(BF16)

        return fn

    tiles_of(d, 384, grad_of(grads[0], z.ea, z.act))
    rs(0, 0)
    ag_wait(2)
    sum_sent(0)
    z.vg[row] = jnp.zeros((8, d), F32)

    def down_back(n):
        i = pick(far_first, n)
        du = dot(z.ea[i], z.wb[2]) * z.der[i].astype(F32)
        z.vg[row, 3:4, :] += jnp.sum(du, axis=0, keepdims=True)
        dub = du.astype(BF16)
        z.der[i] = dub
        z.part[i] = dot(dub, z.wb[1], 1, 1).astype(BF16)
        pl.when(n == 0)(lambda: sum_core(1, z.part, 0))
        pl.when(n == 1)(lambda: sum_cross(1, z.part))
        pl.when(n == 2)(lambda: sum_core(1, z.part, 1))
        pl.when(n >= 1)(lambda: rs(0, n))

    repeat(4, down_back)

    def out_back(n):
        z.act[n] = dot(z.act[n], z.wb[2], 1, 1).astype(BF16)

    repeat(4, out_back)
    rs(0, 4)
    sum_core(2, z.act, 0)
    sum_core(2, z.act, 1)
    ag_sent(2)

    def up_grad(n):
        grad_of(grads[1], z.a2, z.der)(pl.ds(pl.multiple_of(n * 384, 384), 384))
        pl.when(n == 1)(lambda: rs(0, 5))

    repeat(d // 384, up_grad)
    rs(1, 0)
    sum_wait(1, 1)
    sum_wait(1, 2)

    def second_norm(sl):
        da2 = sum_take(1, z.part, sl)
        e = e_ref[sl, :].astype(F32)
        n, inv = normed(z.mid[sl, :])
        dm = e + norm_back(da2 * z.vt[5:6, :], n, inv)
        z.dm[sl, :] = dm
        z.dmb[r, sl, :] = dm.astype(BF16)
        for line, val in ((4, dm), (5, da2 * n), (6, da2), (7, e)):
            z.vg[row, line : line + 1, :] += jnp.sum(val, axis=0, keepdims=True)

    tiles_of(t, 64, second_norm)
    share(3, dms)
    share_sent(0, xa)

    def fins(k, h=None):
        rows = slice(0, nb) if h is None else slice(h * band, (h + 1) * band)
        return lambda i: z.fin.at[k, i, rows]

    def far_ready():
        for h in range(BANDS):
            rs_end(0, h)
        share_relay(3, dms)
        share_wait(3, dms, 2)
        og = dot(z.oq[0, :, 0:q], z.dmb[0], 0, 0)
        for i in range(1, 4):
            og += dot(z.oq[i, :, 0:q], z.dmb[i], 0, 0)
        for i in range(4):
            z.ogs[i, :, 0:q] = og[:, i * q : (i + 1) * q].astype(BF16)
        swap(1, lambda who: z.ogs.at[who])
        z.wo4[r] = z.ogs[r]
        share(4, fins(0))

    def attend_back(n):
        i = pick(near_first, n)
        pl.when(n == 1)(lambda: share_wait(3, dms, 1))
        pl.when(n == 2)(far_ready)
        z.do[:, 0:q] = dot(z.dmb[i], z.wo[...], 1, 1).astype(BF16)
        for h in range(heads):
            qh, kh, vh = (head(i, m, h) for m in range(3))
            g = z.do[:, h * HEAD_DIM : (h + 1) * HEAD_DIM]
            s = dot(qh, kh, 1, 1) * SCALE
            pr = jnp.exp(s - z.lse[i, :, h : h + 1])
            dv = dot(pr.astype(BF16), g, 0, 0)
            dpr = dot(g, vh, 1, 1)
            delta = jnp.sum(pr * dpr, axis=-1, keepdims=True)
            ds = (pr * (dpr - delta) * SCALE).astype(BF16)
            for m, val in enumerate((dot(ds, kh), dot(ds, qh, 0, 0), dv)):
                start = (m + 1) * q + h * HEAD_DIM
                z.xa[i, :, start : start + HEAD_DIM] = val.astype(BF16)
        z.vg[row, 2:3, :] += jnp.sum(z.xa[i].astype(F32), axis=0, keepdims=True)
        pl.when(n == 0)(lambda: rs(0, 6))
        rs(1, n + 1)

    repeat(4, attend_back)
    ag_sent(1)
    sum_sent(1)

    def first_grad(n):
        grad_of(grads[2], z.a1, z.xa)(pl.ds(pl.multiple_of(n * 384, 384), 384))
        pl.when(n == 1)(lambda: rs(1, 5))

    repeat(d // 384, first_grad)
    swap_wait(1)
    for i in range(4):
        grads[2][i * q : (i + 1) * q, 0:q] = z.wo4[i, :, 0:q]
    rs(2, 0)
    rs(1, 6)

    def first_back(n):
        i = pick(far_first, n)
        z.part[i] = dot(z.xa[i, :, q:], z.wb[0, :, q:], 1, 1).astype(BF16)
        pl.when(n == 0)(lambda: sum_core(3, z.part, 0))
        pl.when(n == 1)(lambda: sum_cross(3, z.part))
        pl.when(n == 2)(lambda: sum_core(3, z.part, 1))

    repeat(4, first_back)
    rs(2, 1)
    for h in range(BANDS):
        rs_end(1, h)
    sum_cross(2, z.act)
    share(5, fins(1))
    share_relay(4, fins(0))
    rs(2, 2)
    copies = []

    def put(n, src, dst):
        cp = pltpu.make_async_copy(src, dst, z.out_s.at[n])
        cp.start()
        copies.append(cp)

    for i in (1, 2):
        share_wait(4, fins(0), i)
    put(2, z.fin.at[0], g0_ref)
    rs(2, 3)
    sum_wait(3, 1)
    sum_wait(3, 2)
    share_sent(3, dms)

    def last_norm(sl):
        da1 = sum_take(3, z.part, sl)
        n, inv = normed(x_ref[sl, :].astype(F32))
        z.dmb[r, sl, :] = (z.dm[sl, :] + norm_back(da1 * z.vt[0:1, :], n, inv)).astype(BF16)
        for line, val in ((0, da1 * n), (1, da1)):
            z.vg[row, line : line + 1, :] += jnp.sum(val, axis=0, keepdims=True)

    tiles_of(t, 64, last_norm)
    put(1, z.dmb.at[r], ing_ref)
    small(1, z.vg, 0)
    rs(2, 4)
    small(1, z.vg, 1)
    sum_wait(2, 1)
    sum_wait(2, 2)
    share_sent(2, a2s)

    def last_out(sl):
        z.a2[r, sl, :] = (z.mid[sl, :] + sum_take(2, z.act, sl) + z.vt[7:8, :]).astype(BF16)

    tiles_of(t, 64, last_out)
    put(0, z.a2.at[r], out_ref)
    small(1, z.vg, 2)
    rs(2, 5)
    small(1, z.vg, 3)
    share_relay(5, fins(1))
    small_wait(1, z.vg, 3, 0)
    small_wait(1, z.vg, 2, 1)
    total = z.vg[0]
    for i in range(1, RING):
        total += z.vg[i]
    z.vf[r] = total
    vfs = image_of(z.vf)
    share(6, vfs)
    rs(2, 6)
    for i in (1, 2):
        share_wait(5, fins(1), i)
    put(3, z.fin.at[1], g1_ref)
    for h in range(BANDS):
        rs_end(2, h)
        share(7 + h, fins(2, h))
    share_relay(6, vfs)
    for h in range(BANDS):
        share_relay(7 + h, fins(2, h))
    for i in (1, 2):
        share_wait(6, vfs, i)
    put(5, z.vf, vo_ref)
    for h in range(BANDS):
        for i in (1, 2):
            share_wait(7 + h, fins(2, h), i)
    put(4, z.fin.at[2], g2_ref)
    ag_sent(0)
    for k in range(3):
        rs_sent(k)
    for n, buf in enumerate((z.vb, z.vg)):
        small_sent(n, buf)
        swap_sent(n)
    share_sent(1, ea)
    share_sent(4, fins(0))
    share_sent(5, fins(1))
    share_sent(6, vfs)
    for h in range(BANDS):
        share_sent(7 + h, fins(2, h))
    sum_sent(2)
    sum_sent(3)
    for cp in copies:
        cp.wait()


def finish(q, f, own, shards, d_ref, u_ref, w_ref, v_ref, a_ref, b_ref, *outs):
    qkv_ref, out_ref, up_ref, down_ref, vec_ref, upb_ref, ao_ref, bo_ref, lines = outs
    ao_ref[...] = a_ref[...]
    bo_ref[...] = b_ref[...]
    width = 4 * q
    for i in range(4):
        down_ref[:, i * f : (i + 1) * f] = d_ref[i, :, 0:f].astype(F32)
        up_ref[:, i * f : (i + 1) * f] = u_ref[i, :, 0:f].astype(F32)
        out_ref[:, i * q : (i + 1) * q] = w_ref[i, :, 0:q].astype(F32)
        for k in range(3):
            start = k * width + i * q
            qkv_ref[:, start : start + q] = w_ref[i, :, (k + 1) * q : (k + 2) * q].astype(F32)

    @pl.when(pl.program_id(0) == 0)
    def _():
        lines[...] = v_ref[0] + v_ref[1] + v_ref[2] + v_ref[3]
        for i in range(4):
            upb_ref[:, i * f : (i + 1) * f] = v_ref[i, 3:4, 0:f]
        for i in range(4):
            lines[2:3, i * q : (i + 1) * q] = v_ref[i, 2:3, q : 2 * q]
            lines[3:4, i * q : (i + 1) * q] = v_ref[i, 2:3, 3 * q : 4 * q]
        shard = lax.axis_index("shard")
        for s in range(shards):

            @pl.when(shard == s)
            def _():
                vec_ref[...] = lines[:, s * own : (s + 1) * own]


def per_device(reps, shards, images, cotangent, w_qkv, w_out, w_up, w_down, vectors, up_bias):
    batch, seq, d = images.shape
    hidden = w_up.shape[1]
    q, f = d // reps, hidden // reps
    wide = -(-max(4 * q, f) // 128) * 128
    sub = shards // RING
    groups = [[i * sub + j for j in range(sub)] for i in range(RING)]
    own = d // shards
    weights = (w_qkv, w_out, w_up, w_down, vectors)
    if sub > 1:
        weights = tuple(
            lax.all_gather(w, "shard", axis=0, tiled=True, axis_index_groups=groups) for w in weights
        )
    c = Sizes(d, seq, wide, own * sub, sub, hidden)
    vmem = pl.BlockSpec(memory_space=pltpu.VMEM)
    hbm = pl.BlockSpec(memory_space=pl.ANY)
    grad = jax.ShapeDtypeStruct((4, c.b, wide), BF16)
    tok = jax.ShapeDtypeStruct((seq, d), BF16)
    outputs, input_grad, *terms, vf = pl.pallas_call(
        functools.partial(kernel, c),
        out_shape=(tok, tok, grad, grad, grad, jax.ShapeDtypeStruct((4, 8, d), F32)),
        in_specs=[hbm] * 4 + [vmem] * 4,
        out_specs=(hbm,) * 6,
        scratch_shapes=[make(c) for make in SCRATCH.values()],
        name="layer",
        compiler_params=pltpu.CompilerParams(
            collective_id=0, has_side_effects=True, vmem_limit_bytes=67043328
        ),
    )(*weights[:4], images.reshape(seq, d), cotangent.reshape(seq, d), weights[4].T, up_bias.reshape(1, hidden))
    if sub > 1:
        terms = [
            lax.psum_scatter(
                g.astype(F32), "shard", scatter_dimension=1, tiled=True, axis_index_groups=groups
            )
            for g in terms
        ]
        vf = lax.psum(vf, "shard", axis_index_groups=groups)
    steps = BANDS if own % (16 * BANDS) == 0 else 1
    rows = own // steps
    trow = -(-seq // (16 * steps)) * 16

    def lined(width):
        return pl.BlockSpec((rows, width), lambda j: (j, 0))

    part = pl.BlockSpec((4, rows, wide), lambda j: (0, j, 0))
    toks = pl.BlockSpec((trow, d), lambda j: (j, 0))

    def whole(*shape):
        return pl.BlockSpec(shape, lambda j: (0,) * len(shape))

    def f32(*shape):
        return jax.ShapeDtypeStruct(shape, F32)

    g_qkv, g_out, g_up, g_down, vec, upb, outputs, input_grad = pl.pallas_call(
        functools.partial(finish, q, f, own, shards),
        grid=(steps,),
        out_shape=(
            f32(own, 3 * d), f32(own, d), f32(own, hidden), f32(own, hidden), f32(8, own), f32(1, hidden), tok, tok
        ),
        in_specs=[part] * 3 + [whole(4, 8, d), toks, toks],
        out_specs=(
            lined(3 * d), lined(d), lined(hidden), lined(hidden), whole(8, own), whole(1, hidden), toks, toks
        ),
        scratch_shapes=[pltpu.VMEM((8, d), F32)],
        name="unpack",
    )(*terms, vf, outputs, input_grad)
    shape = (batch, seq, d)
    return (
        outputs.reshape(shape),
        input_grad.reshape(shape),
        g_qkv,
        g_out,
        g_up,
        g_down,
        vec.T,
        upb.reshape(hidden),
    )


def solution(mesh):
    reps, shards = mesh.shape["rep"], mesh.shape["shard"]
    token = P(("rep", "shard"), None, None)
    line = P("shard", None)

    def body(*args):
        return per_device(reps, shards, *args)

    return jax.shard_map(
        body,
        mesh=mesh,
        in_specs=(token, token, line, line, line, line, line, P()),
        out_specs=(token, token, line, line, line, line, line, P()),
        check_vma=False,
    )
```

time: 269 us -> 226 us (0.84)
  local copies, waits for them, and re-layouts: 23.2 us -> 1.32 us
  Pallas kernels: 236 us -> 221 us
  other arithmetic: 5.21 us -> 1.37 us
    pallas_call x1, Pallas kernels: 236 us -> 215 us  [per_device(): pl.pallas_call(functools.partial(kernel, c), out_shape=(tok, tok, grad, g...]
    concatenate x8 -> x0, local copies, waits for them, and re-layouts: 10.4 us -> none  [the longest x2 4.88 us: columns(): return jnp.concatenate([g[i, :, :ffq] for i in range(reps)], axis=1)]
    pallas_call x0 -> x1, Pallas kernels: none -> 6.62 us  [per_device(): pl.pallas_call(functools.partial(finish, q, f, own, shards), grid=(steps,...]
    dynamic_slice x4 -> x0, local copies, waits for them, and re-layouts: 4.19 us -> none  [the longest x2 2.73 us: take(): return lax.dynamic_slice_in_dim(w, start, size, 1)]
    unnamed x7 -> x0, local copies, waits for them, and re-layouts: 3.54 us -> none
    convert_element_type x3 -> x0, other arithmetic: 3.2 us -> none  [finish(): g = g.astype(F32)]
where the time goes in v3:
time: 226 us; the launch traced here: 225 us
  Pallas kernels  221 us (98%)
    pallas_call x1, Pallas kernels, per_device(): pl.pallas_call(functools.partial(kernel, c), out_shape=(tok, tok, grad, g...  215 us
    pallas_call x1, Pallas kernels, per_device(): pl.pallas_call(functools.partial(finish, q, f, own, shards), grid=(steps,...  6.62 us

profile of v3, /device:TPU:0, one launch (start us, length us, event | category | flops | bytes accessed | tf_op | source)
XLA Modules:
  0.0 224.7 jit_solution(1032159560104722142)
XLA Ops:
  0.6 1.3 reshape.36.ub_ref
  2.0 214.7 %layer.1 = (bf16[256,1152]{1,0:T(8,128)(2,1)}, bf16[256,1152]{1,0:T(8,128)(2,1)}, bf16[4,144,1152]{2,1,0:T(8,128)(2,1)}, bf16[4,144,1152]{2,1,0:T(8,128)(2,1)}, ...) custom-call(bf16[144,3456]{1,0:T(8,128)(2,1)} %wq_ref.1, bf16[144,1152]{1,0:T(8,128)(2,1)} %wo_ref.1, ...), custom_call_target="tpu_custom_call" | custom-call | tf_op jit(solution)/shard_map/layer/pallas_call | solution.py:728
  216.7 6.6 %unpack.1 = (f32[144,3456]{1,0:T(8,128)}, f32[144,1152]{1,0:T(8,128)}, f32[144,4304]{1,0:T(8,128)}, f32[144,4304]{1,0:T(8,128)}, f32[8,144]{1,0:T(8,128)}, /*ind...) custom-call(bf16[4,144,1152]{2,1,0:T(8,128)(2,1)} %get-tuple-element.22.d_ref, ...), custom_call_target="tpu_custom_call" | custom-call | tf_op jit(solution)/shard_map/unpack/pallas_call | solution.py:763
  223.3 1.4 reduce
